TPU v7x, 32 devices: a whole 2x2x4 slice. The times are simulated.
32 devices in a mesh: grp: 2 (over x), sp: 16 (over z, y, core).
Axes of the slice: x: 2, y: 2, z: 4, core: 2. Of those that a mesh axis runs over, the one named last changes fastest.
Arguments:
- field: float32 [16, 32, 1024], P('grp', 'sp'), may hold values from -6 to 6
- mix_rate: float32 [32, 1024], P('sp'), may hold values from 0.05 to 2
- react: float32 [16, 16], replicated, may hold values from -1.5 to 1.5
- particles: float32 [16, 262144], P(None, ('grp', 'sp')), may hold values from -6 to 6
- cells: int32 [2, 262144], P(None, ('grp', 'sp')), may hold values from 0 to 2047
- counts: int32 [2048], P(('grp', 'sp')), may hold values from 1 to 128
- dest: int32 [2048], P(('grp', 'sp')), may hold values from 0 to 2, as said below
Outputs:
- field_out: float32 [16, 32, 1024], P('grp', 'sp')
- spread_out: float32 [16, 32, 1024], P('grp', 'sp')
- particles_out: float32 [16, 262144], P(None, ('grp', 'sp'))
Inputs may be any that keep to these rules, and one draw needn't show every extreme that they name: cells[1] refers to the slab that the slot's block reaches after migration. Among each device's 64 blocks exactly 16 have dest 1 and exactly 16 have dest 2.
All inputs are finite; a program needn't handle non-finite values.
Results may differ from a plain program's by a relative error of at most 0.0055.
Values may be sent and summed in bfloat16 or wider, within the bound.
No kernel may reach another device: no remote copies, remote signals or barrier semaphores. Data moves between devices by JAX's collectives and lax.ppermute only.
A program may use at most 64 MiB of HBM per device.

v0:
```python
import jax
import jax.numpy as jnp
from jax import lax
from jax.sharding import PartitionSpec as P

ROW_LENGTH = 32
MOVE = 16


NU_COEF = 0.15
KAPPA = 16.0
REACT_STEP = 0.5


def extended(block, sides, width):
    for axis, dim in sides:
        count = lax.axis_size(axis)
        forward = [(i, i + 1) for i in range(count - 1)]
        forward.append((count - 1, 0))
        backward = [(target, source) for source, target in forward]
        low = lax.ppermute(
            lax.slice_in_dim(block, block.shape[dim] - width, None, axis=dim), axis, forward
        )
        high = lax.ppermute(lax.slice_in_dim(block, 0, width, axis=dim), axis, backward)
        block = jnp.concatenate([low, block, high], axis=dim)
    return block


def from_behind(value, axis, steps):
    count = lax.axis_size(axis)
    pairs = [(source, (source + steps) % count) for source in range(count)]
    return lax.ppermute(value, axis, pairs)


def diffuse(padded):
    field = padded[:, 1:-1]
    neighbour_slabs = padded[:, 2:] + padded[:, :-2]
    neighbour_slabs = neighbour_slabs + jnp.roll(field, 1, axis=2) + jnp.roll(field, -1, axis=2)
    neighbour_slabs = (
        neighbour_slabs + jnp.roll(field, ROW_LENGTH, axis=2) + jnp.roll(field, -ROW_LENGTH, axis=2)
    )
    return field + NU_COEF * (neighbour_slabs - 6.0 * field)


def diffuse_owned(field):
    padded = extended(field, (("sp", 1),), 1)
    return diffuse(padded)


def collect_owned_cells(diffused):
    return lax.all_gather(diffused.astype(jnp.bfloat16), "grp", axis=0, tiled=True)


def combine_owned_sums(moments, width, cells_dev):
    sums = moments[: 2 * width].reshape(2, width, cells_dev)
    owned_sums = lax.psum_scatter(sums, "grp", scatter_dimension=1, tiled=True)
    total_count = lax.psum(moments[2 * width], "grp")
    return (owned_sums, total_count)


def refresh(diffused, sums, count):
    return diffused + (sums[0] - count * diffused) / (count + KAPPA)


def spread_of(diffused, sums, count):
    return (sums[1] - 2.0 * diffused * sums[0] + count * diffused * diffused) / (count + KAPPA)


def live_mask(counts, total):
    blocks_dev = total // 128
    slot = lax.broadcasted_iota(jnp.int32, (blocks_dev, 128), 1)
    return (slot < counts[:, None]).astype(jnp.float32).reshape(total)


def weight_rows(rate_flat):
    weight = 1.0 - jnp.exp(-0.5 * rate_flat)
    upper_part = weight.astype(jnp.bfloat16)
    lower_part = (weight - upper_part.astype(jnp.float32)).astype(jnp.bfloat16)
    return jnp.stack([upper_part, lower_part], 0)


def advance(phi, cell_ids, live, shared_moments, extra_rows, react):
    width, total = phi.shape
    cells_dev = shared_moments.shape[1]
    table = jnp.concatenate([shared_moments, extra_rows], 0)
    span = min(1024, total)
    turns = total // span
    grid = lax.broadcasted_iota(jnp.int32, (cells_dev, 1), 0)

    def one_block(index, carry):
        result, moments = carry
        start = index * span
        piece = lax.dynamic_slice_in_dim(phi, start, span, 1)
        located = lax.dynamic_slice_in_dim(cell_ids, start, span, 0)
        alive = lax.dynamic_slice_in_dim(live, start, span, 0)
        onehot = (grid == located[None, :]).astype(jnp.bfloat16)
        looked = jnp.dot(table, onehot, preferred_element_type=jnp.float32)
        value = looked[:width]
        weight = looked[width] + looked[width + 1]
        mixed = piece + weight * (value - piece)
        stepped = mixed + REACT_STEP * jnp.tanh(
            jnp.dot(react.T, mixed, precision=lax.Precision.HIGHEST)
        )
        kept = alive * stepped
        rows = jnp.concatenate([kept, kept * stepped, alive[None]], 0).astype(jnp.bfloat16)
        deposit = lax.dot_general(
            rows, onehot, (((1,), (1,)), ((), ())), preferred_element_type=jnp.float32
        )
        return (lax.dynamic_update_slice_in_dim(result, stepped, start, 1), moments + deposit)

    initial = (jnp.zeros_like(phi), jnp.zeros((2 * width + 1, cells_dev), jnp.float32))
    return lax.fori_loop(0, turns, one_block, initial)


def migrate(phi, upcoming_cells, counts, dest):
    width, total = phi.shape
    blocks_dev = total // 128
    keep = blocks_dev - 2 * MOVE
    order = jnp.argsort(dest, stable=True)
    blocks = jnp.take(phi.reshape(width, blocks_dev, 128), order, axis=1)
    cell_blocks = jnp.take(upcoming_cells.reshape(blocks_dev, 128), order, axis=0).astype(
        jnp.float32
    )
    packed = jnp.concatenate([blocks, cell_blocks[None]], 0)
    block_sizes = jnp.take(counts, order).astype(jnp.float32)
    from_below = from_behind((packed[:, keep + MOVE :], block_sizes[keep + MOVE :]), "sp", 1)
    from_above = from_behind(
        (packed[:, keep : keep + MOVE], block_sizes[keep : keep + MOVE]), "sp", -1
    )
    merged = jnp.concatenate([packed[:, :keep], from_below[0], from_above[0]], 1)
    new_sizes = jnp.concatenate([block_sizes[:keep], from_below[1], from_above[1]], 0)
    moved = merged[:width].reshape(width, total)
    moved_cells = merged[width].reshape(total).astype(jnp.int32)
    return (moved, moved_cells, new_sizes.astype(jnp.int32))


def shards(field, mix_rate, react, particles, cells, counts, dest):
    owned, depth, plane = field.shape
    width, total = particles.shape
    cells_dev = depth * plane
    extra_rows = weight_rows(mix_rate.reshape(-1))
    live_first = live_mask(counts, total)
    diffused = diffuse_owned(field).reshape(owned, cells_dev)
    shared_moments = collect_owned_cells(diffused)
    stepped, moments = advance(particles, cells[0], live_first, shared_moments, extra_rows, react)
    moved, moved_cells, moved_counts = migrate(stepped, cells[1], counts, dest)
    live_next = live_mask(moved_counts, total)
    owned_sums, total_count = combine_owned_sums(moments, width, cells_dev)
    refreshed = refresh(diffused, owned_sums, total_count).reshape(owned, depth, plane)
    diffused = diffuse_owned(refreshed).reshape(owned, cells_dev)
    shared_moments = collect_owned_cells(diffused)
    final, moments = advance(moved, moved_cells, live_next, shared_moments, extra_rows, react)
    owned_sums, total_count = combine_owned_sums(moments, width, cells_dev)
    field_out = refresh(diffused, owned_sums, total_count).reshape(owned, depth, plane)
    spread_out = spread_of(diffused, owned_sums, total_count).reshape(owned, depth, plane)
    return (field_out, spread_out, live_next[None] * final)


def solution(mesh):
    return jax.shard_map(
        shards,
        mesh=mesh,
        in_specs=(
            P("grp", "sp", None),
            P("sp", None),
            P(),
            P(None, ("grp", "sp")),
            P(None, ("grp", "sp")),
            P(("grp", "sp")),
            P(("grp", "sp")),
        ),
        out_specs=(P("grp", "sp", None), P("grp", "sp", None), P(None, ("grp", "sp"))),
        check_vma=False,
    )
```

profile of v0, /device:TPU:0, one launch (start us, length us, event | category | flops | bytes accessed | tf_op | source)
XLA Modules:
  0.0 145.9 jit_solution(8574681312790705626)
XLA Ops:
  7.3 2.7 %sort.17 = (s32[64]{0:T(128)}, s32[64]{0:T(128)S(1)}) sort(s32[64]{0:T(128)} %param.17, s32[64]{0:T(128)S(1)} %iota.30), dimensions={0}, to_apply=%region_4.5 | sort | flops 384 | bytes 1024 | tf_op jit(solution)/shard_map/jit(argsort)/sort | solution.py:119
  12.0 5.0 %collective-permute-start.7 = (f32[16]{0:T(128)S(1)}, f32[16]{0:T(128)S(1)}, u32[]{:S(2)}, u32[]{:S(2)}) collective-permute-start(f32[16]{0:T(128)S(1)} %get-tuple-element.454), channel_id=1, source_target_pairs={{0,15},{1,0},{2,1},{3,2},{4,3},{5,4},{6,5},{7,6},{8,7},{9,8},{10,9... | collective-permute-start | bytes 200 | tf_op jit(solution)/shard_map/ppermute | solution.py:32
  21.7 3.0 %collective-permute-done.1 = f32[8,1,1024]{2,1,0:T(1,128)S(1)} collective-permute-done((f32[8,1,1024]{2,1,0:T(1,128)S(1)}, f32[8,1,1024]{2,1,0:T(1,128)S(1)}, u32[]{:S(2)}, u32[]{:S(2)}) %collective-permute-start.1) | collective-permute-done | bytes 32800 | tf_op jit(solution)/shard_map/ppermute | solution.py:21
  25.1 4.6 %all_gather.6 = bf16[16,2048]{1,0:T(8,128)(2,1)S(1)} all-gather(bf16[8,2048]{1,0:T(8,128)(2,1)S(1)} %bitcast.88), channel_id=1, replica_groups=mesh['grp'=2,'sp'=16] {'grp'}, dimensions={0}, use_global_device_ids=true | all-gather | bytes 98304 | tf_op jit(solution)/shard_map/all_gather | solution.py:51
  29.7 34.8 %while.32 = (s32[]{:T(128)}, f32[16,8192]{1,0:T(8,128)S(1)}, f32[33,2048]{1,0:T(8,128)S(1)}, f32[16,8192]{1,0:T(8,128)}, s32[8192]{0:T(1024)S(1)}, /*index=5*/bf...) while((s32[]{:T(128)}, f32[16,8192]{1,0:T(8,128)S(1)}, ...), condition=%wide.region_1.2_spmd.clone, body=%wide.region_0.1_spmd.clone.sunk | while | flops 221786112 | bytes 1213629 | solution.py:112
  32.4 1.7 %fusion.100 = f32[33,2048]{1,0:T(8,128)S(1)} fusion(s32[1024]{0:T(1024)S(1)} %dynamic_slice.70, f32[33,2048]{1,0:T(8,128)S(1)} %get-tuple-element.587, pred[]{:T(512)S(6)} %compare.10, bf16[1,1024]{1,0:T(2,128)(2,1)S(1)} %broadcast_in_dim.82, bf16[16,1024]{1,0:T(8,128)(2,1)S(1)} %get-tuple-element.558, bf16[16,1024]{1,0:T(8,128)(2,1)S(1)} %get-tuple-element.559), kind=kOutput, calls=%fused_computation.10.clone.1 | convolution fusion | flops 140847104 | bytes 612353 | tf_op jit(solution)/shard_map/while/body/eval_jaxpr/dot_general | solution.py:106
  36.8 1.7 %fusion.100 = f32[33,2048]{1,0:T(8,128)S(1)} fusion(s32[1024]{0:T(1024)S(1)} %dynamic_slice.70, f32[33,2048]{1,0:T(8,128)S(1)} %get-tuple-element.587, pred[]{:T(512)S(6)} %compare.10, bf16[1,1024]{1,0:T(2,128)(2,1)S(1)} %broadcast_in_dim.82, bf16[16,1024]{1,0:T(8,128)(2,1)S(1)} %get-tuple-element.558, bf16[16,1024]{1,0:T(8,128)(2,1)S(1)} %get-tuple-element.559), kind=kOutput, calls=%fused_computation.10.clone.1 | convolution fusion | flops 140847104 | bytes 612353 | tf_op jit(solution)/shard_map/while/body/eval_jaxpr/dot_general | solution.py:106
  41.1 1.7 %fusion.100 = f32[33,2048]{1,0:T(8,128)S(1)} fusion(s32[1024]{0:T(1024)S(1)} %dynamic_slice.70, f32[33,2048]{1,0:T(8,128)S(1)} %get-tuple-element.587, pred[]{:T(512)S(6)} %compare.10, bf16[1,1024]{1,0:T(2,128)(2,1)S(1)} %broadcast_in_dim.82, bf16[16,1024]{1,0:T(8,128)(2,1)S(1)} %get-tuple-element.558, bf16[16,1024]{1,0:T(8,128)(2,1)S(1)} %get-tuple-element.559), kind=kOutput, calls=%fused_computation.10.clone.1 | convolution fusion | flops 140847104 | bytes 612353 | tf_op jit(solution)/shard_map/while/body/eval_jaxpr/dot_general | solution.py:106
  45.4 1.7 %fusion.100 = f32[33,2048]{1,0:T(8,128)S(1)} fusion(s32[1024]{0:T(1024)S(1)} %dynamic_slice.70, f32[33,2048]{1,0:T(8,128)S(1)} %get-tuple-element.587, pred[]{:T(512)S(6)} %compare.10, bf16[1,1024]{1,0:T(2,128)(2,1)S(1)} %broadcast_in_dim.82, bf16[16,1024]{1,0:T(8,128)(2,1)S(1)} %get-tuple-element.558, bf16[16,1024]{1,0:T(8,128)(2,1)S(1)} %get-tuple-element.559), kind=kOutput, calls=%fused_computation.10.clone.1 | convolution fusion | flops 140847104 | bytes 612353 | tf_op jit(solution)/shard_map/while/body/eval_jaxpr/dot_general | solution.py:106
  49.8 1.7 %fusion.100 = f32[33,2048]{1,0:T(8,128)S(1)} fusion(s32[1024]{0:T(1024)S(1)} %dynamic_slice.70, f32[33,2048]{1,0:T(8,128)S(1)} %get-tuple-element.587, pred[]{:T(512)S(6)} %compare.10, bf16[1,1024]{1,0:T(2,128)(2,1)S(1)} %broadcast_in_dim.82, bf16[16,1024]{1,0:T(8,128)(2,1)S(1)} %get-tuple-element.558, bf16[16,1024]{1,0:T(8,128)(2,1)S(1)} %get-tuple-element.559), kind=kOutput, calls=%fused_computation.10.clone.1 | convolution fusion | flops 140847104 | bytes 612353 | tf_op jit(solution)/shard_map/while/body/eval_jaxpr/dot_general | solution.py:106
  54.1 1.7 %fusion.100 = f32[33,2048]{1,0:T(8,128)S(1)} fusion(s32[1024]{0:T(1024)S(1)} %dynamic_slice.70, f32[33,2048]{1,0:T(8,128)S(1)} %get-tuple-element.587, pred[]{:T(512)S(6)} %compare.10, bf16[1,1024]{1,0:T(2,128)(2,1)S(1)} %broadcast_in_dim.82, bf16[16,1024]{1,0:T(8,128)(2,1)S(1)} %get-tuple-element.558, bf16[16,1024]{1,0:T(8,128)(2,1)S(1)} %get-tuple-element.559), kind=kOutput, calls=%fused_computation.10.clone.1 | convolution fusion | flops 140847104 | bytes 612353 | tf_op jit(solution)/shard_map/while/body/eval_jaxpr/dot_general | solution.py:106
  58.5 1.7 %fusion.100 = f32[33,2048]{1,0:T(8,128)S(1)} fusion(s32[1024]{0:T(1024)S(1)} %dynamic_slice.70, f32[33,2048]{1,0:T(8,128)S(1)} %get-tuple-element.587, pred[]{:T(512)S(6)} %compare.10, bf16[1,1024]{1,0:T(2,128)(2,1)S(1)} %broadcast_in_dim.82, bf16[16,1024]{1,0:T(8,128)(2,1)S(1)} %get-tuple-element.558, bf16[16,1024]{1,0:T(8,128)(2,1)S(1)} %get-tuple-element.559), kind=kOutput, calls=%fused_computation.10.clone.1 | convolution fusion | flops 140847104 | bytes 612353 | tf_op jit(solution)/shard_map/while/body/eval_jaxpr/dot_general | solution.py:106
  62.8 1.7 %fusion.100 = f32[33,2048]{1,0:T(8,128)S(1)} fusion(s32[1024]{0:T(1024)S(1)} %dynamic_slice.70, f32[33,2048]{1,0:T(8,128)S(1)} %get-tuple-element.587, pred[]{:T(512)S(6)} %compare.10, bf16[1,1024]{1,0:T(2,128)(2,1)S(1)} %broadcast_in_dim.82, bf16[16,1024]{1,0:T(8,128)(2,1)S(1)} %get-tuple-element.558, bf16[16,1024]{1,0:T(8,128)(2,1)S(1)} %get-tuple-element.559), kind=kOutput, calls=%fused_computation.10.clone.1 | convolution fusion | flops 140847104 | bytes 612353 | tf_op jit(solution)/shard_map/while/body/eval_jaxpr/dot_general | solution.py:106
  65.4 5.0 %psum.14 = f32[2048]{0:T(1024)S(1)} all-reduce(f32[2048]{0:T(1024)S(1)} %bitcast.97), channel_id=1, replica_groups=mesh['grp'=2,'sp'=16] {'grp'}, use_global_device_ids=true, to_apply=%region_3.4 | all-reduce | flops 2048 | bytes 16384 | tf_op jit(solution)/shard_map/psum | solution.py:57
  70.5 4.4 %collective-permute-start.5 = (f32[17,16,128]{2,0,1:T(8,128)S(1)}, f32[17,16,128]{2,0,1:T(8,128)S(1)}, u32[]{:S(2)}, u32[]{:S(2)}) collective-permute-start(f32[17,16,128]{2,0,1:T(8,128)S(1)} %get-tuple-element.426), channel_id=1, source_target_pairs={{0,15},{1,0},{2,1},{3,2},{4,3},{5,4},{6,5},{7,6},{8,7},{9,8},{10,9... | collective-permute-start | bytes 417800 | tf_op jit(solution)/shard_map/ppermute | solution.py:32
  75.8 2.5 %collective-permute-done.4 = f32[17,16,128]{2,0,1:T(8,128)S(1)} collective-permute-done((f32[17,16,128]{2,0,1:T(8,128)S(1)}, f32[17,16,128]{2,0,1:T(8,128)S(1)}, u32[]{:S(2)}, u32[]{:S(2)}) %collective-permute-start.4) | collective-permute-done | bytes 139296 | tf_op jit(solution)/shard_map/ppermute | solution.py:32
  78.4 6.4 %reduce-scatter.3.cloned.1.call-done = f32[2,8,2048]{2,1,0:T(8,128)} async-done(((f32[2,16,2048]{2,1,0:T(8,128)}), f32[2,8,2048]{2,1,0:T(8,128)}) %reduce-scatter.3.cloned.1.call-update) | async-done | bytes 131088 | tf_op jit(solution)/shard_map/reduce_scatter | solution.py:56
  86.2 3.6 %collective-permute-start.2 = (f32[8,1,1024]{2,1,0:T(1,128)S(1)}, f32[8,1,1024]{2,1,0:T(1,128)S(1)}, u32[]{:S(2)}, u32[]{:S(2)}) collective-permute-start(f32[8,1,1024]{2,1,0:T(1,128)S(1)} %get-tuple-element.433), channel_id=1, source_target_pairs={{1,0},{2,1},{3,2},{4,3},{5,4},{6,5},{7,6},{8,7},{9,8},{10,9},{11,1... | collective-permute-start | bytes 98312 | tf_op jit(solution)/shard_map/ppermute | solution.py:24
  89.9 1.5 %collective-permute-done.2 = f32[8,1,1024]{2,1,0:T(1,128)S(1)} collective-permute-done((f32[8,1,1024]{2,1,0:T(1,128)S(1)}, f32[8,1,1024]{2,1,0:T(1,128)S(1)}, u32[]{:S(2)}, u32[]{:S(2)}) %collective-permute-start.2) | collective-permute-done | bytes 32800 | tf_op jit(solution)/shard_map/ppermute | solution.py:24
  91.4 4.4 %collective-permute-done.3 = f32[8,1,1024]{2,1,0:T(1,128)S(1)} collective-permute-done((f32[8,1,1024]{2,1,0:T(1,128)S(1)}, f32[8,1,1024]{2,1,0:T(1,128)S(1)}, u32[]{:S(2)}, u32[]{:S(2)}) %collective-permute-start.3) | collective-permute-done | bytes 32800 | tf_op jit(solution)/shard_map/ppermute | solution.py:21
  96.1 4.6 %all_gather.7 = bf16[16,2048]{1,0:T(8,128)(2,1)S(1)} all-gather(bf16[8,2048]{1,0:T(8,128)(2,1)S(1)} %bitcast.89), channel_id=1, replica_groups=mesh['grp'=2,'sp'=16] {'grp'}, dimensions={0}, use_global_device_ids=true | all-gather | bytes 98304 | tf_op jit(solution)/shard_map/all_gather | solution.py:51
  100.8 27.5 %while.33 = (s32[]{:T(128)}, f32[16,8192]{1,0:T(8,128)S(1)}, f32[33,2048]{1,0:T(8,128)S(1)}, f32[16,8192]{1,0:T(8,128)S(1)}, s32[8192]{0:T(1024)S(1)}, /*index=5...) while((s32[]{:T(128)}, f32[16,8192]{1,0:T(8,128)S(1)}, ...), condition=%wide.region_6.7_spmd.clone, body=%wide.region_5.6_spmd.clone.sunk | while | flops 221786112 | bytes 1213629 | solution.py:112
  102.5 1.7 %fusion.106 = f32[33,2048]{1,0:T(8,128)S(1)} fusion(s32[1024]{0:T(1024)S(1)} %dynamic_slice.73, f32[33,2048]{1,0:T(8,128)S(1)} %get-tuple-element.623, pred[]{:T(512)S(6)} %compare.11, bf16[1,1024]{1,0:T(2,128)(2,1)S(1)} %broadcast_in_dim.83, bf16[16,1024]{1,0:T(8,128)(2,1)S(1)} %get-tuple-element.571, bf16[16,1024]{1,0:T(8,128)(2,1)S(1)} %get-tuple-element.572), kind=kOutput, calls=%fused_computation.38.clone.1 | convolution fusion | flops 140847104 | bytes 612353 | tf_op jit(solution)/shard_map/while/body/eval_jaxpr/dot_general | solution.py:106
  106.0 1.7 %fusion.106 = f32[33,2048]{1,0:T(8,128)S(1)} fusion(s32[1024]{0:T(1024)S(1)} %dynamic_slice.73, f32[33,2048]{1,0:T(8,128)S(1)} %get-tuple-element.623, pred[]{:T(512)S(6)} %compare.11, bf16[1,1024]{1,0:T(2,128)(2,1)S(1)} %broadcast_in_dim.83, bf16[16,1024]{1,0:T(8,128)(2,1)S(1)} %get-tuple-element.571, bf16[16,1024]{1,0:T(8,128)(2,1)S(1)} %get-tuple-element.572), kind=kOutput, calls=%fused_computation.38.clone.1 | convolution fusion | flops 140847104 | bytes 612353 | tf_op jit(solution)/shard_map/while/body/eval_jaxpr/dot_general | solution.py:106
  109.4 1.7 %fusion.106 = f32[33,2048]{1,0:T(8,128)S(1)} fusion(s32[1024]{0:T(1024)S(1)} %dynamic_slice.73, f32[33,2048]{1,0:T(8,128)S(1)} %get-tuple-element.623, pred[]{:T(512)S(6)} %compare.11, bf16[1,1024]{1,0:T(2,128)(2,1)S(1)} %broadcast_in_dim.83, bf16[16,1024]{1,0:T(8,128)(2,1)S(1)} %get-tuple-element.571, bf16[16,1024]{1,0:T(8,128)(2,1)S(1)} %get-tuple-element.572), kind=kOutput, calls=%fused_computation.38.clone.1 | convolution fusion | flops 140847104 | bytes 612353 | tf_op jit(solution)/shard_map/while/body/eval_jaxpr/dot_general | solution.py:106
  112.8 1.7 %fusion.106 = f32[33,2048]{1,0:T(8,128)S(1)} fusion(s32[1024]{0:T(1024)S(1)} %dynamic_slice.73, f32[33,2048]{1,0:T(8,128)S(1)} %get-tuple-element.623, pred[]{:T(512)S(6)} %compare.11, bf16[1,1024]{1,0:T(2,128)(2,1)S(1)} %broadcast_in_dim.83, bf16[16,1024]{1,0:T(8,128)(2,1)S(1)} %get-tuple-element.571, bf16[16,1024]{1,0:T(8,128)(2,1)S(1)} %get-tuple-element.572), kind=kOutput, calls=%fused_computation.38.clone.1 | convolution fusion | flops 140847104 | bytes 612353 | tf_op jit(solution)/shard_map/while/body/eval_jaxpr/dot_general | solution.py:106
  116.3 1.7 %fusion.106 = f32[33,2048]{1,0:T(8,128)S(1)} fusion(s32[1024]{0:T(1024)S(1)} %dynamic_slice.73, f32[33,2048]{1,0:T(8,128)S(1)} %get-tuple-element.623, pred[]{:T(512)S(6)} %compare.11, bf16[1,1024]{1,0:T(2,128)(2,1)S(1)} %broadcast_in_dim.83, bf16[16,1024]{1,0:T(8,128)(2,1)S(1)} %get-tuple-element.571, bf16[16,1024]{1,0:T(8,128)(2,1)S(1)} %get-tuple-element.572), kind=kOutput, calls=%fused_computation.38.clone.1 | convolution fusion | flops 140847104 | bytes 612353 | tf_op jit(solution)/shard_map/while/body/eval_jaxpr/dot_general | solution.py:106
  119.7 1.7 %fusion.106 = f32[33,2048]{1,0:T(8,128)S(1)} fusion(s32[1024]{0:T(1024)S(1)} %dynamic_slice.73, f32[33,2048]{1,0:T(8,128)S(1)} %get-tuple-element.623, pred[]{:T(512)S(6)} %compare.11, bf16[1,1024]{1,0:T(2,128)(2,1)S(1)} %broadcast_in_dim.83, bf16[16,1024]{1,0:T(8,128)(2,1)S(1)} %get-tuple-element.571, bf16[16,1024]{1,0:T(8,128)(2,1)S(1)} %get-tuple-element.572), kind=kOutput, calls=%fused_computation.38.clone.1 | convolution fusion | flops 140847104 | bytes 612353 | tf_op jit(solution)/shard_map/while/body/eval_jaxpr/dot_general | solution.py:106
  123.1 1.7 %fusion.106 = f32[33,2048]{1,0:T(8,128)S(1)} fusion(s32[1024]{0:T(1024)S(1)} %dynamic_slice.73, f32[33,2048]{1,0:T(8,128)S(1)} %get-tuple-element.623, pred[]{:T(512)S(6)} %compare.11, bf16[1,1024]{1,0:T(2,128)(2,1)S(1)} %broadcast_in_dim.83, bf16[16,1024]{1,0:T(8,128)(2,1)S(1)} %get-tuple-element.571, bf16[16,1024]{1,0:T(8,128)(2,1)S(1)} %get-tuple-element.572), kind=kOutput, calls=%fused_computation.38.clone.1 | convolution fusion | flops 140847104 | bytes 612353 | tf_op jit(solution)/shard_map/while/body/eval_jaxpr/dot_general | solution.py:106
  126.6 1.7 %fusion.106 = f32[33,2048]{1,0:T(8,128)S(1)} fusion(s32[1024]{0:T(1024)S(1)} %dynamic_slice.73, f32[33,2048]{1,0:T(8,128)S(1)} %get-tuple-element.623, pred[]{:T(512)S(6)} %compare.11, bf16[1,1024]{1,0:T(2,128)(2,1)S(1)} %broadcast_in_dim.83, bf16[16,1024]{1,0:T(8,128)(2,1)S(1)} %get-tuple-element.571, bf16[16,1024]{1,0:T(8,128)(2,1)S(1)} %get-tuple-element.572), kind=kOutput, calls=%fused_computation.38.clone.1 | convolution fusion | flops 140847104 | bytes 612353 | tf_op jit(solution)/shard_map/while/body/eval_jaxpr/dot_general | solution.py:106
  129.9 5.1 %psum.15 = f32[2048]{0:T(1024)S(1)} all-reduce(f32[2048]{0:T(1024)S(1)} %bitcast.96), channel_id=1, replica_groups=mesh['grp'=2,'sp'=16] {'grp'}, use_global_device_ids=true, to_apply=%region_8.9 | all-reduce | flops 2048 | bytes 16384 | tf_op jit(solution)/shard_map/psum | solution.py:57
  135.0 2.3 %reduce-scatter.5.cloned.1.call-done = f32[2,8,2048]{2,1,0:T(8,128)} async-done(((f32[2,16,2048]{2,1,0:T(8,128)}), f32[2,8,2048]{2,1,0:T(8,128)}) %reduce-scatter.5.cloned.1.call-update) | async-done | bytes 131088 | tf_op jit(solution)/shard_map/reduce_scatter | solution.py:56
  (181 shorter events, 48.6 us)
Async XLA Ops:
  7.2 13.2 %copy-start = (s32[64]{0:T(128)S(1)}, s32[64]{0:T(128)}, u32[]{:S(2)}) copy-start(s32[64]{0:T(128)} %param.16) | copy-start | bytes 772
  7.2 13.1 %copy-start.1 = (f32[8,2,1024]{2,1,0:T(2,128)S(1)}, f32[8,2,1024]{2,1,0:T(2,128)}, u32[]{:S(2)}) copy-start(f32[8,2,1024]{2,1,0:T(2,128)} %param.11) | copy-start | bytes 196612
  7.2 13.5 %copy-start.3 = (s32[2,8192]{1,0:T(2,128)S(1)}, s32[2,8192]{1,0:T(2,128)}, u32[]{:S(2)}) copy-start(s32[2,8192]{1,0:T(2,128)} %param.15) | copy-start | bytes 196612
  7.2 77.6 %reduce-scatter.3.cloned.1.call-start = ((), (), s32[]{:S(2)}) async-start(), calls=%async_computation.2 | async-start | bytes 393216 | tf_op jit(solution)/shard_map/reduce_scatter | solution.py:56
  11.5 10.1 %collective-permute-start.6 = (f32[16]{0:T(128)S(1)}, f32[16]{0:T(128)S(1)}, u32[]{:S(2)}, u32[]{:S(2)}) collective-permute-start(f32[16]{0:T(128)S(1)} %get-tuple-element.453), channel_id=1, source_target_pairs={{0,1},{1,2},{2,3},{3,4},{4,5},{5,6},{6,7},{7,8},{8,9},{9,10},{10,1... | collective-permute-start | bytes 200 | tf_op jit(solution)/shard_map/ppermute | solution.py:32
  12.0 9.6 %collective-permute-start.7 = (f32[16]{0:T(128)S(1)}, f32[16]{0:T(128)S(1)}, u32[]{:S(2)}, u32[]{:S(2)}) collective-permute-start(f32[16]{0:T(128)S(1)} %get-tuple-element.454), channel_id=1, source_target_pairs={{0,15},{1,0},{2,1},{3,2},{4,3},{5,4},{6,5},{7,6},{8,7},{9,8},{10,9... | collective-permute-start | bytes 200 | tf_op jit(solution)/shard_map/ppermute | solution.py:32
  18.0 3.7 %collective-permute-start = (f32[8,1,1024]{2,1,0:T(1,128)S(1)}, f32[8,1,1024]{2,1,0:T(1,128)S(1)}, u32[]{:S(2)}, u32[]{:S(2)}) collective-permute-start(f32[8,1,1024]{2,1,0:T(1,128)S(1)} %get-tuple-element.443), channel_id=1, source_target_pairs={{1,0},{2,1},{3,2},{4,3},{5,4},{6,5},{7,6},{8,7},{9,8},{10,9},{11,1... | collective-permute-start | bytes 98312 | tf_op jit(solution)/shard_map/ppermute | solution.py:24
  18.7 6.0 %collective-permute-start.1 = (f32[8,1,1024]{2,1,0:T(1,128)S(1)}, f32[8,1,1024]{2,1,0:T(1,128)S(1)}, u32[]{:S(2)}, u32[]{:S(2)}) collective-permute-start(f32[8,1,1024]{2,1,0:T(1,128)S(1)} %get-tuple-element.444), channel_id=1, source_target_pairs={{0,1},{1,2},{2,3},{3,4},{4,5},{5,6},{6,7},{7,8},{8,9},{9,10},{10,1... | collective-permute-start | bytes 98312 | tf_op jit(solution)/shard_map/ppermute | solution.py:21
  21.4 8.3 %copy-start.2 = (f32[16,16]{1,0:T(8,128)S(1)}, f32[16,16]{1,0:T(8,128)}, u32[]{:S(2)}) copy-start(f32[16,16]{1,0:T(8,128)} %param.13) | copy-start | bytes 3076
  70.4 7.8 %collective-permute-start.4 = (f32[17,16,128]{2,0,1:T(8,128)S(1)}, f32[17,16,128]{2,0,1:T(8,128)S(1)}, u32[]{:S(2)}, u32[]{:S(2)}) collective-permute-start(f32[17,16,128]{2,0,1:T(8,128)S(1)} %get-tuple-element.425), channel_id=1, source_target_pairs={{0,1},{1,2},{2,3},{3,4},{4,5},{5,6},{6,7},{7,8},{8,9},{9,10},{10,1... | collective-permute-start | bytes 417800 | tf_op jit(solution)/shard_map/ppermute | solution.py:32
  70.5 7.8 %collective-permute-start.5 = (f32[17,16,128]{2,0,1:T(8,128)S(1)}, f32[17,16,128]{2,0,1:T(8,128)S(1)}, u32[]{:S(2)}, u32[]{:S(2)}) collective-permute-start(f32[17,16,128]{2,0,1:T(8,128)S(1)} %get-tuple-element.426), channel_id=1, source_target_pairs={{0,15},{1,0},{2,1},{3,2},{4,3},{5,4},{6,5},{7,6},{8,7},{9,8},{10,9... | collective-permute-start | bytes 417800 | tf_op jit(solution)/shard_map/ppermute | solution.py:32
  75.7 61.7 %reduce-scatter.5.cloned.1.call-start = ((), (), s32[]{:S(2)}) async-start(), calls=%async_computation.3 | async-start | bytes 393216 | tf_op jit(solution)/shard_map/reduce_scatter | solution.py:56
  86.2 5.2 %collective-permute-start.2 = (f32[8,1,1024]{2,1,0:T(1,128)S(1)}, f32[8,1,1024]{2,1,0:T(1,128)S(1)}, u32[]{:S(2)}, u32[]{:S(2)}) collective-permute-start(f32[8,1,1024]{2,1,0:T(1,128)S(1)} %get-tuple-element.433), channel_id=1, source_target_pairs={{1,0},{2,1},{3,2},{4,3},{5,4},{6,5},{7,6},{8,7},{9,8},{10,9},{11,1... | collective-permute-start | bytes 98312 | tf_op jit(solution)/shard_map/ppermute | solution.py:24
  89.8 6.0 %collective-permute-start.3 = (f32[8,1,1024]{2,1,0:T(1,128)S(1)}, f32[8,1,1024]{2,1,0:T(1,128)S(1)}, u32[]{:S(2)}, u32[]{:S(2)}) collective-permute-start(f32[8,1,1024]{2,1,0:T(1,128)S(1)} %get-tuple-element.434), channel_id=1, source_target_pairs={{0,1},{1,2},{2,3},{3,4},{4,5},{5,6},{6,7},{7,8},{8,9},{9,10},{10,1... | collective-permute-start | bytes 98312 | tf_op jit(solution)/shard_map/ppermute | solution.py:21
Sparse Core Ops, SparseCore 0:
  75.8 9.0 reduce-scatter.2
  129.1 8.1 reduce-scatter.4
where the time goes:
time: 147 us; the launch traced here: 146 us
  matrix products  60.6 us (41%)
  waiting for transfers between devices  20.3 us (14%)
  blocking collectives  19.3 us (13%)
  starting transfers between devices  14.4 us (10%)
  between operations  14.4 us (10%)
  local copies, waits for them, and re-layouts  9.19 us (6%)
  other arithmetic  6.7 us (5%)
    dot_general x16, matrix products, one_block(): lax.dot_general(rows, onehot, (((1,), (1,)), ((), ())), preferred_element...  26.6 us
    dot_general x16, matrix products, one_block(): looked = jnp.dot(table, onehot, preferred_element_type=jnp.float32)  22.3 us
    dot_general x16, matrix products, one_block(): jnp.dot(react.T, mixed, precision=lax.Precision.HIGHEST)  11.6 us
    psum x2, blocking collectives, combine_owned_sums(): total_count = lax.psum(moments[2 * width], 'grp')  10.1 us
    ppermute x4, starting transfers between devices, from_behind(): return lax.ppermute(value, axis, pairs)  10 us
    all_gather x2, blocking collectives, collect_owned_cells(): lax.all_gather(diffused.astype(jnp.bfloat16), 'grp', axis=0, tiled=True)  9.17 us
    reduce_scatter x2, waiting for transfers between devices, combine_owned_sums(): owned_sums = lax.psum_scatter(sums, 'grp', scatter_dimension=1, tiled=True)  8.75 us
    ppermute x2, waiting for transfers between devices, extended(): lax.ppermute(lax.slice_in_dim(block, block.shape[dim] - width, None, axis...  7.45 us
  transfers between devices with their start and end apart: 10, of which 6 were waited for; matrix products, arithmetic and copies ran while one was open for 4% of the time, Pallas kernels for 0%

commit v1 on v0

v1 whole, which is shorter than its diff:
```python
import functools
import jax
import jax.numpy as jnp
from jax import lax
from jax.experimental import pallas as pl
from jax.experimental.pallas import tpu as pltpu
from jax.sharding import PartitionSpec as P

ROW_LENGTH = 32
MOVE = 16
BLOCK = 128
LOW = 256
SPAN = 1024
SPLIT = 128.0

NU_COEF = 0.15
KAPPA = 16.0
REACT_STEP = 0.5
AXES = ("grp", "sp")
BF = jnp.bfloat16
F32 = jnp.float32


def partner(s, pairing, n_sp):
    if pairing is None:
        return s
    if pairing == 0:
        return s ^ 1
    return (((s + 1) ^ 1) - 1) % n_sp


def exchange(value, shift, pairing):
    n_grp, n_sp = lax.axis_size("grp"), lax.axis_size("sp")
    pairs = [
        (g * n_sp + s, ((g + shift) % n_grp) * n_sp + partner(s, pairing, n_sp))
        for g in range(n_grp)
        for s in range(n_sp)
    ]
    return lax.ppermute(value, AXES, pairs)


def pick(options, index):
    result = options[0]
    for position in range(1, len(options)):
        result = jnp.where(index == position, options[position], result)
    return result


def by_owner(pieces, group, n_grp):
    rows = []
    for owner in range(n_grp):
        shift = lax.rem(group - owner + n_grp, n_grp)
        rows.append(pick(pieces, shift))
    return jnp.concatenate(rows, 0) if n_grp > 1 else rows[0]


def spread_step(planes, width):
    inner = planes[width:-width]
    total = planes[2 * width :] + planes[: -2 * width]
    length = planes.shape[1]
    for amount in (1, length - 1, ROW_LENGTH, length - ROW_LENGTH):
        total = total + pltpu.roll(inner, amount, 1)
    return inner + NU_COEF * (total - 6.0 * inner)


def fill_table(table, diffused, width, parts_per_plane, depth):
    for plane in range(depth):
        for part in range(parts_per_plane):
            at = (plane * parts_per_plane + part) * width
            table[at : at + width, :] = diffused[
                plane * width : (plane + 1) * width, part * LOW : (part + 1) * LOW
            ].astype(BF)


def advance_span(phi, code, table, reaction, n_parts, squares):
    width, span = phi.shape
    column = lax.bitwise_and(code, LOW - 1)
    part = lax.shift_right_logical(code, LOW.bit_length() - 1)
    column_grid = lax.broadcasted_iota(jnp.int32, (LOW, span), 0)
    onehot = (column_grid == column).astype(F32).astype(BF)
    looked = jnp.dot(table[...], onehot, preferred_element_type=F32)
    part_rows = jnp.broadcast_to(part, (width, span))
    value = jnp.zeros((width, span), F32)
    for k in range(n_parts):
        value = jnp.where(part_rows == k, looked[k * width : (k + 1) * width], value)
    base = n_parts * width
    part_grid = lax.broadcasted_iota(jnp.int32, (n_parts, span), 0)
    mine = part_grid == part
    weights = looked[base : base + n_parts] + looked[base + n_parts : base + 2 * n_parts]
    weight = jnp.sum(jnp.where(mine, weights, 0.0), 0, keepdims=True)
    mixed = phi + weight * (value - phi)
    upper = mixed.astype(BF)
    lower = (mixed - upper.astype(F32)).astype(BF)
    drive = jnp.dot(
        reaction, jnp.concatenate([upper, lower, upper], 0), preferred_element_type=F32
    )
    stepped = mixed + REACT_STEP * jnp.tanh(drive)
    rows = [stepped, stepped * stepped] if squares else [stepped]
    deposits = []
    for row in rows:
        for k in range(n_parts):
            deposits.append(jnp.where(part_rows == k, row, 0.0).astype(BF))
    deposits.append(jnp.where(mine, 1.0, 0.0).astype(BF))
    sums = lax.dot_general(
        jnp.concatenate(deposits, 0),
        onehot,
        (((1,), (1,)), ((), ())),
        preferred_element_type=F32,
    )
    return stepped, sums


def split_count(count):
    upper = jnp.floor(count * (1.0 / SPLIT))
    return upper, count - upper * SPLIT


def reaction_rows(react):
    turned = react.T
    upper = turned.astype(BF)
    lower = (turned - upper.astype(F32)).astype(BF)
    return jnp.concatenate([upper, upper, lower], 1)


def indices():
    return lax.axis_index("grp"), lax.axis_index("sp")


def order_kernel(dest, counts, particles, cells, rate, sorted_phi, codes, weights):
    _, slab = indices()
    even = lax.rem(slab, 2) == 0
    blocks = particles.shape[1] // BLOCK
    keep = blocks - 2 * MOVE
    cells_dev = rate.shape[0] * rate.shape[1]
    lane = lax.broadcasted_iota(jnp.int32, (2, BLOCK), 1)
    stay = jnp.int32(0)
    below = jnp.where(even, keep + MOVE, keep).astype(jnp.int32)
    above = jnp.where(even, keep, keep + MOVE).astype(jnp.int32)
    for block in range(blocks):
        where = dest[block]
        place = jnp.where(where == 0, stay, jnp.where(where == 1, below, above))
        stay = stay + jnp.where(where == 0, 1, 0)
        below = below + jnp.where(where == 1, 1, 0)
        above = above + jnp.where(where == 2, 1, 0)
        at = pl.ds(pl.multiple_of(place * BLOCK, BLOCK), BLOCK)
        source = slice(block * BLOCK, (block + 1) * BLOCK)
        sorted_phi[:, at] = particles[:, source]
        codes[:, at] = jnp.where(lane < counts[block], cells[:, source], cells_dev)
    depth, plane = rate.shape
    rows = [
        rate[z : z + 1, k * LOW : (k + 1) * LOW]
        for z in range(depth)
        for k in range(plane // LOW)
    ]
    weight = 1.0 - jnp.exp(-0.5 * jnp.concatenate(rows, 0))
    upper = weight.astype(BF)
    lower = (weight - upper.astype(F32)).astype(BF)
    weights[...] = jnp.concatenate([upper, lower], 0)


def first_kernel(n_grp, own, *refs):
    n_in = 5 + 3 * n_grp
    react, sorted_phi, codes, weights, mine = refs[:5]
    fields = refs[5 : n_in - 1]
    (diffused_out, sums_out, slab_msg, pair0_msg, pair1_msg, stay_phi) = refs[n_in - 1 : n_in + 5]
    table = refs[n_in + 5]
    group, slab = indices()
    even = lax.rem(slab, 2) == 0
    width, total = sorted_phi.shape
    depth = mine.shape[0] // own
    plane = mine.shape[1]
    per_plane = plane // LOW
    n_parts = depth * per_plane
    here, low, high = [mine[...]], [], []
    position = 0
    for shift in range(n_grp):
        if shift > 0:
            here.append(fields[position][...].astype(F32))
            position += 1
        one = fields[position][...].astype(F32)
        two = fields[position + 1][...].astype(F32)
        position += 2
        low.append(jnp.where(even, two, one))
        high.append(jnp.where(even, one, two))
    planes = []
    for pieces in (low, here, high):
        for z in range(depth):
            planes.append(
                by_owner([piece[z * own : (z + 1) * own] for piece in pieces], group, n_grp)
            )
    wide = jnp.concatenate(planes[depth - 2 : 2 * depth + 2], 0)
    diffused = spread_step(wide, width)
    diffused_out[...] = diffused
    fill_table(table, diffused[width:-width], width, per_plane, depth)
    table[n_parts * width :, :] = weights[...]
    reaction = reaction_rows(react[...])
    sums_out[...] = jnp.zeros_like(sums_out)

    def body(index, carry):
        at = pl.ds(pl.multiple_of(index * SPAN, SPAN), SPAN)
        stepped, sums = advance_span(
            sorted_phi[:, at], codes[0:1, at], table, reaction, n_parts, False
        )
        stay_phi[:, at] = stepped
        sums_out[...] += sums
        return carry

    lax.fori_loop(0, total // SPAN, body, 0)
    sums = sums_out[...]
    first = sums[: n_parts * width]
    upper, lower = split_count(sums[n_parts * width :])
    digits = jnp.concatenate([upper, lower], 0).astype(BF)
    n_first = n_parts * width
    slab_msg[:n_first, :] = first.astype(BF)
    slab_msg[n_first:, :] = digits
    half = per_plane * width
    bottom = first[:half].astype(BF)
    top = first[n_first - half :].astype(BF)
    keep = total - 2 * MOVE * BLOCK
    for message, face, start in (
        (pair0_msg, jnp.where(even, top, bottom), keep),
        (pair1_msg, jnp.where(even, bottom, top), keep + MOVE * BLOCK),
    ):
        message[:half, :] = face
        message[half : half + 2 * n_parts, :] = digits
        row = half + 2 * n_parts
        pieces = MOVE * BLOCK // LOW
        columns, parts = [], []
        for k in range(pieces):
            at = slice(start + k * LOW, start + (k + 1) * LOW)
            message[row + k * width : row + (k + 1) * width, :] = stay_phi[:, at].astype(BF)
            code = codes[1:2, at]
            columns.append(lax.bitwise_and(code, LOW - 1).astype(F32))
            parts.append(lax.shift_right_logical(code, LOW.bit_length() - 1).astype(F32))
        row += pieces * width
        message[row : row + 2 * pieces, :] = jnp.concatenate(columns + parts, 0).astype(BF)


def second_kernel(n_grp, own, *refs):
    n_in = 6 + 3 * n_grp - 1
    react, stay_phi, codes, weights, diffused0, sums0 = refs[:6]
    received = refs[6:n_in]
    particles_out, own_sums, own_diffused = refs[n_in : n_in + 3]
    messages = refs[n_in + 3 : n_in + 2 + n_grp]
    table, phi, code_row, refreshed, sums = refs[n_in + 2 + n_grp :]
    group, slab = indices()
    even = lax.rem(slab, 2) == 0
    width, total = stay_phi.shape
    n_parts = weights.shape[0] // 2
    n_first = n_parts * width
    plane = diffused0.shape[1]
    per_plane = plane // LOW
    depth = n_parts // per_plane
    half = per_plane * width
    keep = total - 2 * MOVE * BLOCK
    pieces = MOVE * BLOCK // LOW

    here_first, here_count = sums0[:n_first], sums0[n_first:]
    side_first, side_count = [None, None], [None, None]
    position = 0
    moving = [None, None]
    for shift in range(n_grp):
        if shift > 0:
            slab_rows = received[position][...].astype(F32)
            position += 1
            here_first = here_first + slab_rows[:n_first]
            here_count = (
                here_count
                + slab_rows[n_first : n_first + n_parts] * SPLIT
                + slab_rows[n_first + n_parts :]
            )
        for pairing in range(2):
            message = received[position]
            position += 1
            rows = message[: half + 2 * n_parts, :].astype(F32)
            first = rows[:half]
            count = rows[half : half + n_parts] * SPLIT + rows[half + n_parts :]
            if shift == 0:
                moving[pairing] = message
                side_first[pairing], side_count[pairing] = first, count
            else:
                side_first[pairing] = side_first[pairing] + first
                side_count[pairing] = side_count[pairing] + count
    low_first = jnp.where(even, side_first[1], side_first[0])
    high_first = jnp.where(even, side_first[0], side_first[1])
    low_count = jnp.where(even, side_count[1], side_count[0])
    high_count = jnp.where(even, side_count[0], side_count[1])
    firsts = [low_first] + [here_first[z * half : (z + 1) * half] for z in range(depth)]
    firsts.append(high_first)
    counts = [low_count[n_parts - per_plane :]]
    counts += [here_count[z * per_plane : (z + 1) * per_plane] for z in range(depth)]
    counts.append(high_count[:per_plane])
    for z in range(depth + 2):
        for k in range(per_plane):
            at = slice(k * LOW, (k + 1) * LOW)
            old = diffused0[z * width : (z + 1) * width, at]
            count = counts[z][k : k + 1]
            change = firsts[z][k * width : (k + 1) * width] - count * old
            refreshed[z * width : (z + 1) * width, at] = old + change / (count + KAPPA)
    diffused = spread_step(refreshed[...], width)
    fill_table(table, diffused, width, per_plane, depth)
    table[n_first:, :] = weights[...]
    for z in range(depth):
        for k in range(per_plane):
            options = [
                diffused[z * width + j * own : z * width + (j + 1) * own, k * LOW : (k + 1) * LOW]
                for j in range(n_grp)
            ]
            at = (z * per_plane + k) * own
            own_diffused[at : at + own, :] = pick(options, group)

    phi[:, :keep] = stay_phi[:, :keep]
    code_row[:, :keep] = codes[1:2, :keep]
    starts = (
        jnp.where(even, keep + MOVE * BLOCK, keep),
        jnp.where(even, keep, keep + MOVE * BLOCK),
    )
    for pairing in range(2):
        message = moving[pairing]
        row = half + 2 * n_parts
        tail = message[row + pieces * width : row + pieces * width + 2 * pieces, :].astype(F32)
        code = (tail[:pieces] + tail[pieces:] * float(LOW)).astype(jnp.int32)
        for k in range(pieces):
            at = pl.ds(pl.multiple_of(starts[pairing] + k * LOW, LOW), LOW)
            phi[:, at] = message[row + k * width : row + (k + 1) * width, :].astype(F32)
            code_row[:, at] = code[k : k + 1]

    reaction = reaction_rows(react[...])
    sums[...] = jnp.zeros_like(sums)

    def body(index, carry):
        at = pl.ds(pl.multiple_of(index * SPAN, SPAN), SPAN)
        code = code_row[:, at]
        stepped, more = advance_span(phi[:, at], code, table, reaction, n_parts, True)
        particles_out[:, at] = jnp.where(code < n_parts * LOW, stepped, 0.0)
        sums[...] += more
        return carry

    lax.fori_loop(0, total // SPAN, body, 0)
    upper, lower = split_count(sums[2 * n_first :, :])
    digits = jnp.concatenate([upper, lower], 0).astype(BF)

    def owned(owner):
        rows = []
        for kind in range(2):
            for k in range(n_parts):
                base = kind * n_first + k * width
                rows.append(
                    pick(
                        [sums[base + j * own : base + (j + 1) * own, :] for j in range(n_grp)],
                        owner,
                    )
                )
        return jnp.concatenate(rows, 0)

    n_own = 2 * n_parts * own
    own_sums[:n_own, :] = owned(group)
    own_sums[n_own:, :] = sums[2 * n_first :, :]
    for shift in range(1, n_grp):
        message = messages[shift - 1]
        message[:n_own, :] = owned(lax.rem(group + shift, n_grp)).astype(BF)
        message[n_own:, :] = digits


def last_kernel(n_grp, own, *refs):
    own_sums, diffused = refs[:2]
    received = refs[2 : 1 + n_grp]
    field_out, spread_out = refs[1 + n_grp :]
    n_parts = diffused.shape[0] // own
    n_half = n_parts * own
    sums = own_sums[: 2 * n_half, :]
    count = own_sums[2 * n_half :, :]
    for message in received:
        rows = message[...].astype(F32)
        sums = sums + rows[: 2 * n_half]
        count = (
            count
            + rows[2 * n_half : 2 * n_half + n_parts] * SPLIT
            + rows[2 * n_half + n_parts :]
        )
    depth = field_out.shape[1]
    per_plane = n_parts // depth
    for z in range(depth):
        for k in range(per_plane):
            at = (z * per_plane + k) * own
            mean = diffused[at : at + own, :]
            first = sums[at : at + own]
            second = sums[n_half + at : n_half + at + own]
            here = count[z * per_plane + k : z * per_plane + k + 1]
            scale = 1.0 / (here + KAPPA)
            columns = slice(k * LOW, (k + 1) * LOW)
            field_out[:, z, columns] = mean + (first - here * mean) * scale
            spread_out[:, z, columns] = (
                second - 2.0 * mean * first + here * mean * mean
            ) * scale


def call(kernel, name, outs, scratch, flops, smem=0, limit=20):
    specs = [pl.BlockSpec(memory_space=pltpu.SMEM)] * smem

    def run(*args):
        return pl.pallas_call(
            kernel,
            out_shape=[jax.ShapeDtypeStruct(shape, dtype) for shape, dtype in outs],
            in_specs=specs + [pl.BlockSpec(memory_space=pltpu.VMEM)] * (len(args) - smem),
            out_specs=[pl.BlockSpec(memory_space=pltpu.VMEM)] * len(outs),
            scratch_shapes=[pltpu.VMEM(shape, dtype) for shape, dtype in scratch],
            compiler_params=pltpu.CompilerParams(vmem_limit_bytes=limit << 20),
            cost_estimate=pl.CostEstimate(flops=flops, bytes_accessed=1 << 20, transcendentals=0),
            name=name,
        )(*args)

    return run


def shards(field, mix_rate, react, particles, cells, counts, dest):
    n_grp = lax.axis_size("grp")
    own, depth, plane = field.shape
    width, total = particles.shape
    n_parts = depth * plane // LOW
    per_plane = plane // LOW
    n_first = n_parts * width
    half = per_plane * width
    pieces = MOVE * BLOCK // LOW

    mine = jnp.transpose(field, (1, 0, 2)).reshape(depth * own, plane)
    sent = mine.astype(BF)
    fields = []
    for shift in range(n_grp):
        if shift > 0:
            fields.append(exchange(sent, shift, None))
        fields.append(exchange(sent, shift, 0))
        fields.append(exchange(sent, shift, 1))
    sorted_phi, codes, weights = call(
        order_kernel,
        "order",
        [((width, total), F32), ((2, total), jnp.int32), ((2 * n_parts, LOW), BF)],
        [],
        1 << 24,
        smem=2,
        limit=8,
    )(dest, counts, particles, cells, mix_rate)

    pair_rows = half + 2 * n_parts + pieces * width + 2 * pieces
    table = ((n_first + 2 * n_parts, LOW), BF)
    diffused0, sums0, slab_msg, pair0_msg, pair1_msg, stay_phi = call(
        functools.partial(first_kernel, n_grp, own),
        "first",
        [
            (((depth + 2) * width, plane), F32),
            ((n_first + n_parts, LOW), F32),
            ((n_first + 2 * n_parts, LOW), BF),
            ((pair_rows, LOW), BF),
            ((pair_rows, LOW), BF),
            ((width, total), F32),
        ],
        [table],
        1 << 32,
    )(react, sorted_phi, codes, weights, mine, *fields)

    received = []
    faces = [message[: half + 2 * n_parts] for message in (pair0_msg, pair1_msg)]
    for shift in range(n_grp):
        if shift > 0:
            received.append(exchange(slab_msg, shift, None))
        for pairing, message in enumerate((pair0_msg, pair1_msg)):
            received.append(exchange(faces[pairing] if shift > 0 else message, shift, pairing))

    n_own = 2 * n_parts * own
    outs = call(
        functools.partial(second_kernel, n_grp, own),
        "second",
        [((width, total), F32), ((n_own + n_parts, LOW), F32), ((n_parts * own, LOW), F32)]
        + [((n_own + 2 * n_parts, LOW), BF)] * (n_grp - 1),
        [
            table,
            ((width, total), F32),
            ((1, total), jnp.int32),
            (((depth + 2) * width, plane), F32),
            ((2 * n_first + n_parts, LOW), F32),
        ],
        1 << 32,
    )(react, stay_phi, codes, weights, diffused0, sums0, *received)
    particles_out, own_sums, own_diffused = outs[:3]
    final = [exchange(outs[2 + shift], shift, None) for shift in range(1, n_grp)]
    field_out, spread_out = call(
        functools.partial(last_kernel, n_grp, own),
        "last",
        [(field.shape, F32), (field.shape, F32)],
        [],
        1 << 20,
        limit=8,
    )(own_sums, own_diffused, *final)
    return field_out, spread_out, particles_out


def solution(mesh):
    return jax.shard_map(
        shards,
        mesh=mesh,
        in_specs=(
            P("grp", "sp", None),
            P("sp", None),
            P(),
            P(None, ("grp", "sp")),
            P(None, ("grp", "sp")),
            P(("grp", "sp")),
            P(("grp", "sp")),
        ),
        out_specs=(P("grp", "sp", None), P("grp", "sp", None), P(None, ("grp", "sp"))),
        check_vma=False,
    )
```

time: 147 us -> 42.7 us (0.29)
  matrix products: 60.6 us -> 0 us
  blocking collectives: 19.3 us -> 0 us
  Pallas kernels: 0 us -> 14.7 us
  between operations: 14.4 us -> 0.79 us
  waiting for transfers between devices: 20.3 us -> 9.8 us
  local copies, waits for them, and re-layouts: 9.19 us -> 2.03 us
  other arithmetic: 6.7 us -> 0 us
    dot_general x48 -> x0, matrix products: 60.6 us -> none  [the longest x16 26.6 us: one_block(): lax.dot_general(rows, onehot, (((1,), (1,)), ((), ())), preferred_element...]
    pallas_call x0 -> x4, Pallas kernels: none -> 14.7 us  [run(): pl.pallas_call(kernel, out_shape=[jax.ShapeDtypeStruct(shape, dtype) for...]
    psum x2 -> x0, blocking collectives: 10.1 us -> none  [combine_owned_sums(): total_count = lax.psum(moments[2 * width], 'grp')]
    all_gather x2 -> x0, blocking collectives: 9.17 us -> none  [collect_owned_cells(): lax.all_gather(diffused.astype(jnp.bfloat16), 'grp', axis=0, tiled=True)]
    reduce_scatter x2 -> x0, waiting for transfers between devices: 8.75 us -> none  [combine_owned_sums(): owned_sums = lax.psum_scatter(sums, 'grp', scatter_dimension=1, tiled=True)]
    slice x18 -> x2, local copies, waits for them, and re-layouts: 5.86 us -> 0.01 us  [shards(): faces = [message[:half + 2 * n_parts] for message in (pair0_msg, pair1_msg)]]
    sort x1 -> x0, other arithmetic: 2.69 us -> none  [migrate(): order = jnp.argsort(dest, stable=True)]
    gather x3 -> x0, local copies, waits for them, and re-layouts: 2.66 us -> none  [the longest x1 1.43 us: migrate(): block_sizes = jnp.take(counts, order).astype(jnp.float32)]
  transfers between devices with their start and end apart: 10 -> 11, of which waited for: 6 -> 3; matrix products, arithmetic and copies ran while one was open for 4% -> 0% of each run, Pallas kernels for 0% -> 3%
where the time goes in v1:
time: 42.7 us; the launch traced here: 42.5 us
  starting transfers between devices  15.2 us (36%)
  Pallas kernels  14.7 us (34%)
  waiting for transfers between devices  9.8 us (23%)
  local copies, waits for them, and re-layouts  2.03 us (5%)
  between operations  0.79 us (2%)
    ppermute x11, starting transfers between devices, exchange(): return lax.ppermute(value, AXES, pairs)  15.2 us
    pallas_call x4, Pallas kernels, run(): pl.pallas_call(kernel, out_shape=[jax.ShapeDtypeStruct(shape, dtype) for...  14.7 us
    ppermute x11, waiting for transfers between devices, exchange(): return lax.ppermute(value, AXES, pairs)  9.8 us
    unnamed x14, local copies, waits for them, and re-layouts  1.07 us
    transpose x2, local copies, waits for them, and re-layouts, shards(): mine = jnp.transpose(field, (1, 0, 2)).reshape(depth * own, plane)  0.95 us
  transfers between devices with their start and end apart: 11, of which 3 were waited for; matrix products, arithmetic and copies ran while one was open for 0% of the time, Pallas kernels for 3%

profile of v1, /device:TPU:0, one launch (start us, length us, event | category | flops | bytes accessed | tf_op | source)
XLA Modules:
  0.0 42.5 jit_solution(13733556282562646892)
XLA Ops:
  0.6 0.9 %copy.15 = bf16[2,8,1024]{2,1,0:T(8,128)(2,1)S(1)} copy(f32[2,8,1024]{2,0,1:T(2,128)} %bitcast.8) | data formatting | bytes 98304 | tf_op jit(solution)/shard_map/transpose | solution.py:426
  1.6 0.0 copy-start.1
  1.6 0.0 copy-start.2
  1.6 0.0 copy-start.3
  1.6 0.0 copy-start.4
  1.6 6.5 %collective-permute-start.4 = (bf16[16,1024]{1,0:T(8,128)(2,1)S(1)}, bf16[16,1024]{1,0:T(8,128)(2,1)S(1)}, u32[]{:S(2)}, u32[]{:S(2)}) collective-permute-start(bf16[16,1024]{1,0:T(8,128)(2,1)S(1)} %bitcast.10), channel_id=1, source_target_pairs={{0,31},{1,18},{2,17},{3,20},{4,19},{5,22},{6,21},{7,24},{8,23},{9,... | collective-permute-start | bytes 98312 | tf_op jit(solution)/shard_map/ppermute | solution.py:39
  8.1 0.0 collective-permute-start.3
  8.1 0.5 %collective-permute-start.2 = (bf16[16,1024]{1,0:T(8,128)(2,1)S(1)}, bf16[16,1024]{1,0:T(8,128)(2,1)S(1)}, u32[]{:S(2)}, u32[]{:S(2)}) collective-permute-start(bf16[16,1024]{1,0:T(8,128)(2,1)S(1)} %bitcast.12), channel_id=1, source_target_pairs={{0,16},{1,17},{2,18},{3,19},{4,20},{5,21},{6,22},{7,23},{8,24},{9,... | collective-permute-start | bytes 98312 | tf_op jit(solution)/shard_map/ppermute | solution.py:39
  8.6 1.4 %collective-permute-start.1 = (bf16[16,1024]{1,0:T(8,128)(2,1)S(1)}, bf16[16,1024]{1,0:T(8,128)(2,1)S(1)}, u32[]{:S(2)}, u32[]{:S(2)}) collective-permute-start(bf16[16,1024]{1,0:T(8,128)(2,1)S(1)} %bitcast.13), channel_id=1, source_target_pairs={{0,15},{1,2},{2,1},{3,4},{4,3},{5,6},{6,5},{7,8},{8,7},{9,10},{10,... | collective-permute-start | bytes 98312 | tf_op jit(solution)/shard_map/ppermute | solution.py:39
  10.1 0.0 collective-permute-start
  10.1 0.0 copy-start
  10.1 1.0 %copy-done = f32[16,8192]{1,0:T(8,128)S(1)} copy-done((f32[16,8192]{1,0:T(8,128)S(1)}, f32[16,8192]{1,0:T(8,128)}, u32[]{:S(2)}) %copy-start) | copy-done | bytes 524312
  11.2 1.1 %order.1 = (f32[16,8192]{1,0:T(8,128)S(1)}, s32[2,8192]{1,0:T(2,128)S(1)}, bf16[16,256]{1,0:T(8,128)(2,1)S(1)}) custom-call(s32[64]{0:T(128)S(1)} %copy-done.3, s32[64]{0:T(128)S(1)} %copy-done.4, f32[16,8192]{1,0:T(8,128)S(1)} %copy-done, s32[2,8192]{1,0:T(2,128)S(1)} %copy-done.1, f32[2,1024]{1,0:T(2,128)S(1)} %copy-done.2), custom_call_target="tpu_custom_call" | custom-call | flops 16777216 | bytes 1048576 | tf_op jit(solution)/shard_map/order/pallas_call | solution.py:402
  12.3 0.0 collective-permute-done.4.refs_9_
  12.3 0.0 collective-permute-done.3.refs_8_
  12.3 0.0 collective-permute-done.2.refs_7_
  12.3 2.4 %collective-permute-done.1.refs_6_ = bf16[16,1024]{1,0:T(8,128)(2,1)S(1)} collective-permute-done((bf16[16,1024]{1,0:T(8,128)(2,1)S(1)}, bf16[16,1024]{1,0:T(8,128)(2,1)S(1)}, u32[]{:S(2)}, u32[]{:S(2)}) %collective-permute-start.1) | collective-permute-done | bytes 32800 | tf_op jit(solution)/shard_map/ppermute | solution.py:39
  14.7 0.0 collective-permute-done.refs_5_
  14.7 6.0 %first.1 = (f32[64,1024]{1,0:T(8,128)S(1)}, f32[136,256]{1,0:T(8,128)S(1)}, bf16[144,256]{1,0:T(8,128)(2,1)S(1)}, bf16[224,256]{1,0:T(8,128)(2,1)S(1)}, bf16[224...) custom-call(f32[16,16]{1,0:T(8,128)S(1)} %copy-done.5, f32[16,8192]{1,0:T(8,128)S(1)} %get-tuple-element.18.refs_1_, ...), custom_call_target="tpu_custom_call" | custom-call | flops 4294967296 | bytes 1048576 | tf_op jit(solution)/shard_map/first/pallas_call | solution.py:402
  20.7 0.1 collective-permute-start.5
  20.8 1.5 %collective-permute-start.6 = (bf16[224,256]{1,0:T(8,128)(2,1)S(1)}, bf16[224,256]{1,0:T(8,128)(2,1)S(1)}, u32[]{:S(2)}, u32[]{:S(2)}) collective-permute-start(bf16[224,256]{1,0:T(8,128)(2,1)S(1)} %get-tuple-element.25), channel_id=1, source_target_pairs={{0,15},{1,2},{2,1},{3,4},{4,3},{5,6},{6,5},{7,8},{8,7},{9,10},{10,... | collective-permute-start | bytes 344072 | tf_op jit(solution)/shard_map/ppermute | solution.py:39
  22.3 1.2 %collective-permute-start.7 = (bf16[144,256]{1,0:T(8,128)(2,1)S(1)}, bf16[144,256]{1,0:T(8,128)(2,1)S(1)}, u32[]{:S(2)}, u32[]{:S(2)}) collective-permute-start(bf16[144,256]{1,0:T(8,128)(2,1)S(1)} %get-tuple-element.26), channel_id=1, source_target_pairs={{0,16},{1,17},{2,18},{3,19},{4,20},{5,21},{6,22},{7,23},{8,24},{9,... | collective-permute-start | bytes 221192 | tf_op jit(solution)/shard_map/ppermute | solution.py:39
  23.5 3.1 %collective-permute-start.9 = (bf16[80,256]{1,0:T(8,128)(2,1)S(1)}, bf16[80,256]{1,0:T(8,128)(2,1)S(1)}, u32[]{:S(2)}, u32[]{:S(2)}) collective-permute-start(bf16[80,256]{1,0:T(8,128)(2,1)S(1)} %slice.7), channel_id=1, source_target_pairs={{0,31},{1,18},{2,17},{3,20},{4,19},{5,22},{6,21},{7,24},{8,23},{9,... | collective-permute-start | bytes 122888 | tf_op jit(solution)/shard_map/ppermute | solution.py:39
  26.5 0.0 collective-permute-start.8
  26.6 4.0 %collective-permute-done.9.refs_10_ = bf16[80,256]{1,0:T(8,128)(2,1)S(1)} collective-permute-done((bf16[80,256]{1,0:T(8,128)(2,1)S(1)}, bf16[80,256]{1,0:T(8,128)(2,1)S(1)}, u32[]{:S(2)}, u32[]{:S(2)}) %collective-permute-start.9) | collective-permute-done | bytes 40992 | tf_op jit(solution)/shard_map/ppermute | solution.py:39
  30.5 0.0 collective-permute-done.8.refs_9_
  30.5 0.0 collective-permute-done.7.refs_8_
  30.6 0.0 collective-permute-done.5.refs_6_
  30.6 6.8 %second.1 = (f32[16,8192]{1,0:T(8,128)}, f32[136,256]{1,0:T(8,128)S(1)}, f32[64,256]{1,0:T(8,128)S(1)}, bf16[144,256]{1,0:T(8,128)(2,1)S(1)}) custom-call(f32[16,16]{1,0:T(8,128)S(1)} %copy-done.5, f32[16,8192]{1,0:T(8,128)S(1)} %get-tuple-element.21.refs_1_, s32[2,8192]{1,0:T(2,128)S(1)} %get-tuple-element.19.refs_2_, ...), custom_call_target="tpu_custom_call" | custom-call | flops 4294967296 | bytes 1048576 | tf_op jit(solution)/shard_map/second/pallas_call | solution.py:402
  37.4 0.9 %collective-permute-start.10 = (bf16[144,256]{1,0:T(8,128)(2,1)S(1)}, bf16[144,256]{1,0:T(8,128)(2,1)S(1)}, u32[]{:S(2)}, u32[]{:S(2)}) collective-permute-start(bf16[144,256]{1,0:T(8,128)(2,1)S(1)} %get-tuple-element.29), channel_id=1, source_target_pairs={{0,16},{1,17},{2,18},{3,19},{4,20},{5,21},{6,22},{7,23},{8,24},{9,... | collective-permute-start | bytes 221192 | tf_op jit(solution)/shard_map/ppermute | solution.py:39
  38.3 3.4 %collective-permute-done.10.refs_2_ = bf16[144,256]{1,0:T(8,128)(2,1)S(1)} collective-permute-done((bf16[144,256]{1,0:T(8,128)(2,1)S(1)}, bf16[144,256]{1,0:T(8,128)(2,1)S(1)}, u32[]{:S(2)}, u32[]{:S(2)}) %collective-permute-start.10) | collective-permute-done | bytes 73760 | tf_op jit(solution)/shard_map/ppermute | solution.py:39
  41.8 0.7 %last.1 = (f32[8,2,1024]{2,1,0:T(2,128)}, f32[8,2,1024]{2,1,0:T(2,128)}) custom-call(f32[136,256]{1,0:T(8,128)S(1)} %get-tuple-element.27.refs_0_, f32[64,256]{1,0:T(8,128)S(1)} %get-tuple-element.28.refs_1_, bf16[144,256]{1,0:T(8,128)(2,1)S(1)} %collective-permute-done.10.refs_2_), custom_call_target="tpu_custom_call" | custom-call | flops 1048576 | bytes 1048576 | tf_op jit(solution)/shard_map/last/pallas_call | solution.py:402
  (12 shorter events, 0.0 us)
Async XLA Ops:
  0.6 9.4 %copy-start.6 = (f32[8,2,1024]{2,1,0:T(2,128)S(1)}, f32[8,2,1024]{2,1,0:T(2,128)}, u32[]{:S(2)}) copy-start(f32[8,2,1024]{2,1,0:T(2,128)} %param.7) | copy-start | bytes 196612
  1.6 8.5 %copy-start.1 = (s32[2,8192]{1,0:T(2,128)S(1)}, s32[2,8192]{1,0:T(2,128)}, u32[]{:S(2)}) copy-start(s32[2,8192]{1,0:T(2,128)} %cells.1) | copy-start | bytes 196612
  1.6 8.5 %copy-start.2 = (f32[2,1024]{1,0:T(2,128)S(1)}, f32[2,1024]{1,0:T(2,128)}, u32[]{:S(2)}) copy-start(f32[2,1024]{1,0:T(2,128)} %rate.1) | copy-start | bytes 24580
  1.6 8.5 %copy-start.3 = (s32[64]{0:T(128)S(1)}, s32[64]{0:T(128)}, u32[]{:S(2)}) copy-start(s32[64]{0:T(128)} %dest.1) | copy-start | bytes 772
  1.6 8.5 %copy-start.4 = (s32[64]{0:T(128)S(1)}, s32[64]{0:T(128)}, u32[]{:S(2)}) copy-start(s32[64]{0:T(128)} %counts.1) | copy-start | bytes 772
  1.6 10.7 %collective-permute-start.4 = (bf16[16,1024]{1,0:T(8,128)(2,1)S(1)}, bf16[16,1024]{1,0:T(8,128)(2,1)S(1)}, u32[]{:S(2)}, u32[]{:S(2)}) collective-permute-start(bf16[16,1024]{1,0:T(8,128)(2,1)S(1)} %bitcast.10), channel_id=1, source_target_pairs={{0,31},{1,18},{2,17},{3,20},{4,19},{5,22},{6,21},{7,24},{8,23},{9,... | collective-permute-start | bytes 98312 | tf_op jit(solution)/shard_map/ppermute | solution.py:39
  8.1 4.2 %collective-permute-start.3 = (bf16[16,1024]{1,0:T(8,128)(2,1)S(1)}, bf16[16,1024]{1,0:T(8,128)(2,1)S(1)}, u32[]{:S(2)}, u32[]{:S(2)}) collective-permute-start(bf16[16,1024]{1,0:T(8,128)(2,1)S(1)} %bitcast.11), channel_id=1, source_target_pairs={{0,17},{1,16},{2,19},{3,18},{4,21},{5,20},{6,23},{7,22},{8,25},{9,... | collective-permute-start | bytes 98312 | tf_op jit(solution)/shard_map/ppermute | solution.py:39
  8.1 4.2 %collective-permute-start.2 = (bf16[16,1024]{1,0:T(8,128)(2,1)S(1)}, bf16[16,1024]{1,0:T(8,128)(2,1)S(1)}, u32[]{:S(2)}, u32[]{:S(2)}) collective-permute-start(bf16[16,1024]{1,0:T(8,128)(2,1)S(1)} %bitcast.12), channel_id=1, source_target_pairs={{0,16},{1,17},{2,18},{3,19},{4,20},{5,21},{6,22},{7,23},{8,24},{9,... | collective-permute-start | bytes 98312 | tf_op jit(solution)/shard_map/ppermute | solution.py:39
  8.6 6.0 %collective-permute-start.1 = (bf16[16,1024]{1,0:T(8,128)(2,1)S(1)}, bf16[16,1024]{1,0:T(8,128)(2,1)S(1)}, u32[]{:S(2)}, u32[]{:S(2)}) collective-permute-start(bf16[16,1024]{1,0:T(8,128)(2,1)S(1)} %bitcast.13), channel_id=1, source_target_pairs={{0,15},{1,2},{2,1},{3,4},{4,3},{5,6},{6,5},{7,8},{8,7},{9,10},{10,... | collective-permute-start | bytes 98312 | tf_op jit(solution)/shard_map/ppermute | solution.py:39
  10.1 4.6 %collective-permute-start = (bf16[16,1024]{1,0:T(8,128)(2,1)S(1)}, bf16[16,1024]{1,0:T(8,128)(2,1)S(1)}, u32[]{:S(2)}, u32[]{:S(2)}) collective-permute-start(bf16[16,1024]{1,0:T(8,128)(2,1)S(1)} %bitcast.14), channel_id=1, source_target_pairs={{0,1},{1,0},{2,3},{3,2},{4,5},{5,4},{6,7},{7,6},{8,9},{9,8},{10,11... | collective-permute-start | bytes 98312 | tf_op jit(solution)/shard_map/ppermute | solution.py:39
  10.1 1.0 %copy-start = (f32[16,8192]{1,0:T(8,128)S(1)}, f32[16,8192]{1,0:T(8,128)}, u32[]{:S(2)}) copy-start(f32[16,8192]{1,0:T(8,128)} %particles.1) | copy-start | bytes 1572868
  11.2 3.5 %copy-start.5 = (f32[16,16]{1,0:T(8,128)S(1)}, f32[16,16]{1,0:T(8,128)}, u32[]{:S(2)}) copy-start(f32[16,16]{1,0:T(8,128)} %refs_0_.3) | copy-start | bytes 3076
  20.7 9.9 %collective-permute-start.5 = (bf16[224,256]{1,0:T(8,128)(2,1)S(1)}, bf16[224,256]{1,0:T(8,128)(2,1)S(1)}, u32[]{:S(2)}, u32[]{:S(2)}) collective-permute-start(bf16[224,256]{1,0:T(8,128)(2,1)S(1)} %get-tuple-element.24), channel_id=1, source_target_pairs={{0,1},{1,0},{2,3},{3,2},{4,5},{5,4},{6,7},{7,6},{8,9},{9,8},{10,11... | collective-permute-start | bytes 344072 | tf_op jit(solution)/shard_map/ppermute | solution.py:39
  20.8 9.8 %collective-permute-start.6 = (bf16[224,256]{1,0:T(8,128)(2,1)S(1)}, bf16[224,256]{1,0:T(8,128)(2,1)S(1)}, u32[]{:S(2)}, u32[]{:S(2)}) collective-permute-start(bf16[224,256]{1,0:T(8,128)(2,1)S(1)} %get-tuple-element.25), channel_id=1, source_target_pairs={{0,15},{1,2},{2,1},{3,4},{4,3},{5,6},{6,5},{7,8},{8,7},{9,10},{10,... | collective-permute-start | bytes 344072 | tf_op jit(solution)/shard_map/ppermute | solution.py:39
  22.3 8.3 %collective-permute-start.7 = (bf16[144,256]{1,0:T(8,128)(2,1)S(1)}, bf16[144,256]{1,0:T(8,128)(2,1)S(1)}, u32[]{:S(2)}, u32[]{:S(2)}) collective-permute-start(bf16[144,256]{1,0:T(8,128)(2,1)S(1)} %get-tuple-element.26), channel_id=1, source_target_pairs={{0,16},{1,17},{2,18},{3,19},{4,20},{5,21},{6,22},{7,23},{8,24},{9,... | collective-permute-start | bytes 221192 | tf_op jit(solution)/shard_map/ppermute | solution.py:39
  23.5 7.1 %collective-permute-start.9 = (bf16[80,256]{1,0:T(8,128)(2,1)S(1)}, bf16[80,256]{1,0:T(8,128)(2,1)S(1)}, u32[]{:S(2)}, u32[]{:S(2)}) collective-permute-start(bf16[80,256]{1,0:T(8,128)(2,1)S(1)} %slice.7), channel_id=1, source_target_pairs={{0,31},{1,18},{2,17},{3,20},{4,19},{5,22},{6,21},{7,24},{8,23},{9,... | collective-permute-start | bytes 122888 | tf_op jit(solution)/shard_map/ppermute | solution.py:39
  26.5 4.0 %collective-permute-start.8 = (bf16[80,256]{1,0:T(8,128)(2,1)S(1)}, bf16[80,256]{1,0:T(8,128)(2,1)S(1)}, u32[]{:S(2)}, u32[]{:S(2)}) collective-permute-start(bf16[80,256]{1,0:T(8,128)(2,1)S(1)} %slice.6), channel_id=1, source_target_pairs={{0,17},{1,16},{2,19},{3,18},{4,21},{5,20},{6,23},{7,22},{8,25},{9,... | collective-permute-start | bytes 122888 | tf_op jit(solution)/shard_map/ppermute | solution.py:39
  37.4 4.4 %collective-permute-start.10 = (bf16[144,256]{1,0:T(8,128)(2,1)S(1)}, bf16[144,256]{1,0:T(8,128)(2,1)S(1)}, u32[]{:S(2)}, u32[]{:S(2)}) collective-permute-start(bf16[144,256]{1,0:T(8,128)(2,1)S(1)} %get-tuple-element.29), channel_id=1, source_target_pairs={{0,16},{1,17},{2,18},{3,19},{4,20},{5,21},{6,22},{7,23},{8,24},{9,... | collective-permute-start | bytes 221192 | tf_op jit(solution)/shard_map/ppermute | solution.py:39

commit v2 on v1

--- a/solution.py
+++ b/solution.py
@@ -10,7 +10,9 @@
 MOVE = 16
 BLOCK = 128
 LOW = 256
-SPAN = 1024
+SPAN = 4096
+UNROLL = True
+STEPS = 2
 SPLIT = 128.0
 
 NU_COEF = 0.15
@@ -72,20 +74,22 @@
             ].astype(BF)
 
 
-def advance_span(phi, code, table, reaction, n_parts, squares):
+def onehot(column):
+    grid = lax.broadcasted_iota(jnp.int32, (LOW, column.shape[1]), 0).astype(F32).astype(BF)
+    return jnp.where(grid == column.astype(BF), jnp.ones((), BF), jnp.zeros((), BF))
+
+
+def produce(phi, code, table, reaction, n_parts):
     width, span = phi.shape
-    column = lax.bitwise_and(code, LOW - 1)
     part = lax.shift_right_logical(code, LOW.bit_length() - 1)
-    column_grid = lax.broadcasted_iota(jnp.int32, (LOW, span), 0)
-    onehot = (column_grid == column).astype(F32).astype(BF)
-    looked = jnp.dot(table[...], onehot, preferred_element_type=F32)
+    column = lax.bitwise_and(code, LOW - 1).astype(F32)
+    looked = jnp.dot(table[...], onehot(column), preferred_element_type=F32)
     part_rows = jnp.broadcast_to(part, (width, span))
-    value = jnp.zeros((width, span), F32)
-    for k in range(n_parts):
+    value = looked[:width]
+    for k in range(1, n_parts):
         value = jnp.where(part_rows == k, looked[k * width : (k + 1) * width], value)
     base = n_parts * width
-    part_grid = lax.broadcasted_iota(jnp.int32, (n_parts, span), 0)
-    mine = part_grid == part
+    mine = lax.broadcasted_iota(jnp.int32, (n_parts, span), 0) == part
     weights = looked[base : base + n_parts] + looked[base + n_parts : base + 2 * n_parts]
     weight = jnp.sum(jnp.where(mine, weights, 0.0), 0, keepdims=True)
     mixed = phi + weight * (value - phi)
@@ -94,20 +98,67 @@
     drive = jnp.dot(
         reaction, jnp.concatenate([upper, lower, upper], 0), preferred_element_type=F32
     )
-    stepped = mixed + REACT_STEP * jnp.tanh(drive)
-    rows = [stepped, stepped * stepped] if squares else [stepped]
-    deposits = []
-    for row in rows:
-        for k in range(n_parts):
-            deposits.append(jnp.where(part_rows == k, row, 0.0).astype(BF))
-    deposits.append(jnp.where(mine, 1.0, 0.0).astype(BF))
-    sums = lax.dot_general(
-        jnp.concatenate(deposits, 0),
-        onehot,
+    return mixed + REACT_STEP * jnp.tanh(drive)
+
+
+def consume(stepped, cell, n_parts, squares, sums):
+    width, span = stepped.shape
+    part = jnp.floor(cell * (1.0 / LOW))
+    column = cell - part * LOW
+    part_rows = jnp.broadcast_to(part.astype(BF), (width, span))
+    masks = [part_rows == jnp.asarray(k, BF) for k in range(n_parts)]
+    left = []
+    for row in [stepped, stepped * stepped] if squares else [stepped]:
+        narrow = row.astype(BF)
+        left += [jnp.where(mask, narrow, jnp.zeros((), BF)) for mask in masks]
+    rank = lax.broadcasted_iota(jnp.int32, (width, span), 0).astype(F32).astype(BF)
+    left.append(jnp.where(rank == part_rows, jnp.ones((), BF), jnp.zeros((), BF)))
+    sums[...] += lax.dot_general(
+        jnp.concatenate(left, 0),
+        onehot(column),
         (((1,), (1,)), ((), ())),
         preferred_element_type=F32,
     )
-    return stepped, sums
+
+
+def advance(phi, codes, code_row, cells, table, reaction, n_parts, squares, mask_dead, out, sums):
+    spans = phi.shape[1] // SPAN
+
+    def span_at(index):
+        if isinstance(index, int):
+            return slice(index * SPAN, (index + 1) * SPAN)
+        return pl.ds(pl.multiple_of(index * SPAN, SPAN), SPAN)
+
+    def make(index):
+        at = span_at(index)
+        code = codes[code_row : code_row + 1, at]
+        stepped = produce(phi[:, at], code, table, reaction, n_parts)
+        out[:, at] = jnp.where(code < n_parts * LOW, stepped, 0.0) if mask_dead else stepped
+
+    def take(index):
+        at = span_at(index)
+        consume(out[:, at], cells[:, at], n_parts, squares, sums)
+
+    sums[...] = jnp.zeros_like(sums)
+    make(0)
+    if UNROLL:
+        for index in range(1, spans):
+            make(index)
+            take(index - 1)
+    else:
+
+        def body(index, carry):
+            for step in range(STEPS):
+                make(STEPS * index + step + 1)
+                take(STEPS * index + step)
+            return carry
+
+        trips = (spans - 1) // STEPS
+        lax.fori_loop(0, trips, body, 0)
+        for index in range(trips * STEPS + 1, spans):
+            make(index)
+            take(index - 1)
+    take(spans - 1)
 
 
 def split_count(count):
@@ -126,7 +177,7 @@
     return lax.axis_index("grp"), lax.axis_index("sp")
 
 
-def order_kernel(dest, counts, particles, cells, rate, sorted_phi, codes, weights):
+def order_kernel(dest, counts, particles, cells, rate, sorted_phi, codes, cells_f, weights):
     _, slab = indices()
     even = lax.rem(slab, 2) == 0
     blocks = particles.shape[1] // BLOCK
@@ -145,7 +196,9 @@
         at = pl.ds(pl.multiple_of(place * BLOCK, BLOCK), BLOCK)
         source = slice(block * BLOCK, (block + 1) * BLOCK)
         sorted_phi[:, at] = particles[:, source]
-        codes[:, at] = jnp.where(lane < counts[block], cells[:, source], cells_dev)
+        code = jnp.where(lane < counts[block], cells[:, source], cells_dev)
+        codes[:, at] = code
+        cells_f[:, at] = code[0:1].astype(F32)
     depth, plane = rate.shape
     rows = [
         rate[z : z + 1, k * LOW : (k + 1) * LOW]
@@ -159,11 +212,11 @@
 
 
 def first_kernel(n_grp, own, *refs):
-    n_in = 5 + 3 * n_grp
-    react, sorted_phi, codes, weights, mine = refs[:5]
-    fields = refs[5 : n_in - 1]
+    n_in = 6 + 3 * n_grp
+    react, sorted_phi, codes, cells_f, weights, mine = refs[:6]
+    fields = refs[6 : n_in - 1]
     (diffused_out, sums_out, slab_msg, pair0_msg, pair1_msg, stay_phi) = refs[n_in - 1 : n_in + 5]
-    table = refs[n_in + 5]
+    table, sums_all = refs[n_in + 5 : n_in + 7]
     group, slab = indices()
     even = lax.rem(slab, 2) == 0
     width, total = sorted_phi.shape
@@ -194,18 +247,10 @@
     fill_table(table, diffused[width:-width], width, per_plane, depth)
     table[n_parts * width :, :] = weights[...]
     reaction = reaction_rows(react[...])
-    sums_out[...] = jnp.zeros_like(sums_out)
-
-    def body(index, carry):
-        at = pl.ds(pl.multiple_of(index * SPAN, SPAN), SPAN)
-        stepped, sums = advance_span(
-            sorted_phi[:, at], codes[0:1, at], table, reaction, n_parts, False
-        )
-        stay_phi[:, at] = stepped
-        sums_out[...] += sums
-        return carry
-
-    lax.fori_loop(0, total // SPAN, body, 0)
+    advance(
+        sorted_phi, codes, 0, cells_f, table, reaction, n_parts, False, False, stay_phi, sums_all
+    )
+    sums_out[...] = sums_all[: (width + 1) * n_parts, :]
     sums = sums_out[...]
     first = sums[: n_parts * width]
     upper, lower = split_count(sums[n_parts * width :])
@@ -225,15 +270,15 @@
         message[half : half + 2 * n_parts, :] = digits
         row = half + 2 * n_parts
         pieces = MOVE * BLOCK // LOW
-        columns, parts = [], []
+        tails, parts = [], []
         for k in range(pieces):
             at = slice(start + k * LOW, start + (k + 1) * LOW)
             message[row + k * width : row + (k + 1) * width, :] = stay_phi[:, at].astype(BF)
             code = codes[1:2, at]
-            columns.append(lax.bitwise_and(code, LOW - 1).astype(F32))
+            tails.append(lax.bitwise_and(code, LOW - 1).astype(F32))
             parts.append(lax.shift_right_logical(code, LOW.bit_length() - 1).astype(F32))
         row += pieces * width
-        message[row : row + 2 * pieces, :] = jnp.concatenate(columns + parts, 0).astype(BF)
+        message[row : row + 2 * pieces, :] = jnp.concatenate(tails + parts, 0).astype(BF)
 
 
 def second_kernel(n_grp, own, *refs):
@@ -242,7 +287,7 @@
     received = refs[6:n_in]
     particles_out, own_sums, own_diffused = refs[n_in : n_in + 3]
     messages = refs[n_in + 3 : n_in + 2 + n_grp]
-    table, phi, code_row, refreshed, sums = refs[n_in + 2 + n_grp :]
+    table, phi, code_row, cells_f, refreshed, sums = refs[n_in + 2 + n_grp :]
     group, slab = indices()
     even = lax.rem(slab, 2) == 0
     width, total = stay_phi.shape
@@ -311,6 +356,7 @@
 
     phi[:, :keep] = stay_phi[:, :keep]
     code_row[:, :keep] = codes[1:2, :keep]
+    cells_f[:, :keep] = codes[1:2, :keep].astype(F32)
     starts = (
         jnp.where(even, keep + MOVE * BLOCK, keep),
         jnp.where(even, keep, keep + MOVE * BLOCK),
@@ -319,25 +365,19 @@
         message = moving[pairing]
         row = half + 2 * n_parts
         tail = message[row + pieces * width : row + pieces * width + 2 * pieces, :].astype(F32)
-        code = (tail[:pieces] + tail[pieces:] * float(LOW)).astype(jnp.int32)
+        cell = tail[:pieces] + tail[pieces:] * float(LOW)
+        code = cell.astype(jnp.int32)
         for k in range(pieces):
             at = pl.ds(pl.multiple_of(starts[pairing] + k * LOW, LOW), LOW)
             phi[:, at] = message[row + k * width : row + (k + 1) * width, :].astype(F32)
             code_row[:, at] = code[k : k + 1]
+            cells_f[:, at] = cell[k : k + 1]
 
     reaction = reaction_rows(react[...])
-    sums[...] = jnp.zeros_like(sums)
-
-    def body(index, carry):
-        at = pl.ds(pl.multiple_of(index * SPAN, SPAN), SPAN)
-        code = code_row[:, at]
-        stepped, more = advance_span(phi[:, at], code, table, reaction, n_parts, True)
-        particles_out[:, at] = jnp.where(code < n_parts * LOW, stepped, 0.0)
-        sums[...] += more
-        return carry
-
-    lax.fori_loop(0, total // SPAN, body, 0)
-    upper, lower = split_count(sums[2 * n_first :, :])
+    advance(
+        phi, code_row, 0, cells_f, table, reaction, n_parts, True, True, particles_out, sums
+    )
+    upper, lower = split_count(sums[2 * n_first : 2 * n_first + n_parts, :])
     digits = jnp.concatenate([upper, lower], 0).astype(BF)
 
     def owned(owner):
@@ -355,7 +395,7 @@
 
     n_own = 2 * n_parts * own
     own_sums[:n_own, :] = owned(group)
-    own_sums[n_own:, :] = sums[2 * n_first :, :]
+    own_sums[n_own:, :] = sums[2 * n_first : 2 * n_first + n_parts, :]
     for shift in range(1, n_grp):
         message = messages[shift - 1]
         message[:n_own, :] = owned(lax.rem(group + shift, n_grp)).astype(BF)
@@ -388,9 +428,9 @@
             second = sums[n_half + at : n_half + at + own]
             here = count[z * per_plane + k : z * per_plane + k + 1]
             scale = 1.0 / (here + KAPPA)
-            columns = slice(k * LOW, (k + 1) * LOW)
-            field_out[:, z, columns] = mean + (first - here * mean) * scale
-            spread_out[:, z, columns] = (
+            cells_f = slice(k * LOW, (k + 1) * LOW)
+            field_out[:, z, cells_f] = mean + (first - here * mean) * scale
+            spread_out[:, z, cells_f] = (
                 second - 2.0 * mean * first + here * mean * mean
             ) * scale
 
@@ -431,10 +471,15 @@
             fields.append(exchange(sent, shift, None))
         fields.append(exchange(sent, shift, 0))
         fields.append(exchange(sent, shift, 1))
-    sorted_phi, codes, weights = call(
+    sorted_phi, codes, cells_f, weights = call(
         order_kernel,
         "order",
-        [((width, total), F32), ((2, total), jnp.int32), ((2 * n_parts, LOW), BF)],
+        [
+            ((width, total), F32),
+            ((2, total), jnp.int32),
+            ((1, total), F32),
+            ((2 * n_parts, LOW), BF),
+        ],
         [],
         1 << 24,
         smem=2,
@@ -454,9 +499,9 @@
             ((pair_rows, LOW), BF),
             ((width, total), F32),
         ],
-        [table],
+        [table, ((n_first + width, LOW), F32)],
         1 << 32,
-    )(react, sorted_phi, codes, weights, mine, *fields)
+    )(react, sorted_phi, codes, cells_f, weights, mine, *fields)
 
     received = []
     faces = [message[: half + 2 * n_parts] for message in (pair0_msg, pair1_msg)]
@@ -476,8 +521,9 @@
             table,
             ((width, total), F32),
             ((1, total), jnp.int32),
+            ((1, total), F32),
             (((depth + 2) * width, plane), F32),
-            ((2 * n_first + n_parts, LOW), F32),
+            ((2 * n_first + width, LOW), F32),
         ],
         1 << 32,
     )(react, stay_phi, codes, weights, diffused0, sums0, *received)

time: 42.7 us -> 35.9 us (0.84)
  Pallas kernels: 14.7 us -> 7.2 us
  waiting for transfers between devices: 9.8 us -> 10.8 us
    pallas_call x4, Pallas kernels: 14.7 us -> 7.2 us  [run(): pl.pallas_call(kernel, out_shape=[jax.ShapeDtypeStruct(shape, dtype) for...]
    ppermute x11, waiting for transfers between devices: 9.8 us -> 10.8 us  [exchange(): return lax.ppermute(value, AXES, pairs)]
where the time goes in v2:
time: 35.9 us; the launch traced here: 35.7 us
  starting transfers between devices  14.9 us (42%)
  waiting for transfers between devices  10.8 us (30%)
  Pallas kernels  7.2 us (20%)
  local copies, waits for them, and re-layouts  2.03 us (6%)
  between operations  0.8 us (2%)
    ppermute x11, starting transfers between devices, exchange(): return lax.ppermute(value, AXES, pairs)  14.9 us
    ppermute x11, waiting for transfers between devices, exchange(): return lax.ppermute(value, AXES, pairs)  10.8 us
    pallas_call x4, Pallas kernels, run(): pl.pallas_call(kernel, out_shape=[jax.ShapeDtypeStruct(shape, dtype) for...  7.2 us
    unnamed x14, local copies, waits for them, and re-layouts  1.07 us
    transpose x2, local copies, waits for them, and re-layouts, shards(): mine = jnp.transpose(field, (1, 0, 2)).reshape(depth * own, plane)  0.95 us
  transfers between devices with their start and end apart: 11, of which 3 were waited for; matrix products, arithmetic and copies ran while one was open for 0% of the time, Pallas kernels for 3%

profile of v2, /device:TPU:0, one launch (start us, length us, event | category | flops | bytes accessed | tf_op | source)
XLA Modules:
  0.0 35.7 jit_solution(7665118091422719142)
XLA Ops:
  0.6 0.9 %copy.15 = bf16[2,8,1024]{2,1,0:T(8,128)(2,1)S(1)} copy(f32[2,8,1024]{2,0,1:T(2,128)} %bitcast.8) | data formatting | bytes 98304 | tf_op jit(solution)/shard_map/transpose | solution.py:466
  1.6 0.0 copy-start.1
  1.6 0.0 copy-start.2
  1.6 0.0 copy-start.3
  1.6 0.0 copy-start.4
  1.6 6.5 %collective-permute-start.4 = (bf16[16,1024]{1,0:T(8,128)(2,1)S(1)}, bf16[16,1024]{1,0:T(8,128)(2,1)S(1)}, u32[]{:S(2)}, u32[]{:S(2)}) collective-permute-start(bf16[16,1024]{1,0:T(8,128)(2,1)S(1)} %bitcast.10), channel_id=1, source_target_pairs={{0,31},{1,18},{2,17},{3,20},{4,19},{5,22},{6,21},{7,24},{8,23},{9,... | collective-permute-start | bytes 98312 | tf_op jit(solution)/shard_map/ppermute | solution.py:41
  8.1 0.0 collective-permute-start.3
  8.1 0.5 %collective-permute-start.2 = (bf16[16,1024]{1,0:T(8,128)(2,1)S(1)}, bf16[16,1024]{1,0:T(8,128)(2,1)S(1)}, u32[]{:S(2)}, u32[]{:S(2)}) collective-permute-start(bf16[16,1024]{1,0:T(8,128)(2,1)S(1)} %bitcast.12), channel_id=1, source_target_pairs={{0,16},{1,17},{2,18},{3,19},{4,20},{5,21},{6,22},{7,23},{8,24},{9,... | collective-permute-start | bytes 98312 | tf_op jit(solution)/shard_map/ppermute | solution.py:41
  8.6 1.4 %collective-permute-start.1 = (bf16[16,1024]{1,0:T(8,128)(2,1)S(1)}, bf16[16,1024]{1,0:T(8,128)(2,1)S(1)}, u32[]{:S(2)}, u32[]{:S(2)}) collective-permute-start(bf16[16,1024]{1,0:T(8,128)(2,1)S(1)} %bitcast.13), channel_id=1, source_target_pairs={{0,15},{1,2},{2,1},{3,4},{4,3},{5,6},{6,5},{7,8},{8,7},{9,10},{10,... | collective-permute-start | bytes 98312 | tf_op jit(solution)/shard_map/ppermute | solution.py:41
  10.1 0.0 collective-permute-start
  10.1 0.0 copy-start
  10.1 1.0 %copy-done = f32[16,8192]{1,0:T(8,128)S(1)} copy-done((f32[16,8192]{1,0:T(8,128)S(1)}, f32[16,8192]{1,0:T(8,128)}, u32[]{:S(2)}) %copy-start) | copy-done | bytes 524312
  11.2 1.1 %order.1 = (f32[16,8192]{1,0:T(8,128)S(1)}, s32[2,8192]{1,0:T(2,128)S(1)}, f32[1,8192]{1,0:T(1,128)S(1)}, bf16[16,256]{1,0:T(8,128)(2,1)S(1)}) custom-call(s32[64]{0:T(128)S(1)} %copy-done.3, s32[64]{0:T(128)S(1)} %copy-done.4, f32[16,8192]{1,0:T(8,128)S(1)} %copy-done, s32[2,8192]{1,0:T(2,128)S(1)} %copy-done.1, f32[2,1024]{1,0:T(2,128)S(1)} %copy-done.2), custom_call_target="tpu_custom_call" | custom-call | flops 16777216 | bytes 1048576 | tf_op jit(solution)/shard_map/order/pallas_call | solution.py:442
  12.3 0.0 copy-start.5
  12.3 0.0 collective-permute-done.4.refs_10_
  12.3 0.0 collective-permute-done.3.refs_9_
  12.3 0.0 collective-permute-done.2.refs_8_
  12.4 2.3 %collective-permute-done.1.refs_7_ = bf16[16,1024]{1,0:T(8,128)(2,1)S(1)} collective-permute-done((bf16[16,1024]{1,0:T(8,128)(2,1)S(1)}, bf16[16,1024]{1,0:T(8,128)(2,1)S(1)}, u32[]{:S(2)}, u32[]{:S(2)}) %collective-permute-start.1) | collective-permute-done | bytes 32800 | tf_op jit(solution)/shard_map/ppermute | solution.py:41
  14.7 2.7 %first.1 = (f32[64,1024]{1,0:T(8,128)S(1)}, f32[136,256]{1,0:T(8,128)S(1)}, bf16[144,256]{1,0:T(8,128)(2,1)S(1)}, bf16[224,256]{1,0:T(8,128)(2,1)S(1)}, bf16[224...) custom-call(f32[16,16]{1,0:T(8,128)S(1)} %copy-done.5, f32[16,8192]{1,0:T(8,128)S(1)} %get-tuple-element.19.refs_1_, ...), custom_call_target="tpu_custom_call" | custom-call | flops 4294967296 | bytes 1048576 | tf_op jit(solution)/shard_map/first/pallas_call | solution.py:442
  17.4 0.1 collective-permute-start.5
  17.5 1.8 %collective-permute-start.6 = (bf16[224,256]{1,0:T(8,128)(2,1)S(1)}, bf16[224,256]{1,0:T(8,128)(2,1)S(1)}, u32[]{:S(2)}, u32[]{:S(2)}) collective-permute-start(bf16[224,256]{1,0:T(8,128)(2,1)S(1)} %get-tuple-element.27), channel_id=1, source_target_pairs={{0,15},{1,2},{2,1},{3,4},{4,3},{5,6},{6,5},{7,8},{8,7},{9,10},{10,... | collective-permute-start | bytes 344072 | tf_op jit(solution)/shard_map/ppermute | solution.py:41
  19.3 1.5 %collective-permute-start.7 = (bf16[144,256]{1,0:T(8,128)(2,1)S(1)}, bf16[144,256]{1,0:T(8,128)(2,1)S(1)}, u32[]{:S(2)}, u32[]{:S(2)}) collective-permute-start(bf16[144,256]{1,0:T(8,128)(2,1)S(1)} %get-tuple-element.28), channel_id=1, source_target_pairs={{0,16},{1,17},{2,18},{3,19},{4,20},{5,21},{6,22},{7,23},{8,24},{9,... | collective-permute-start | bytes 221192 | tf_op jit(solution)/shard_map/ppermute | solution.py:41
  20.8 2.4 %collective-permute-start.9 = (bf16[80,256]{1,0:T(8,128)(2,1)S(1)}, bf16[80,256]{1,0:T(8,128)(2,1)S(1)}, u32[]{:S(2)}, u32[]{:S(2)}) collective-permute-start(bf16[80,256]{1,0:T(8,128)(2,1)S(1)} %slice.7), channel_id=1, source_target_pairs={{0,31},{1,18},{2,17},{3,20},{4,19},{5,22},{6,21},{7,24},{8,23},{9,... | collective-permute-start | bytes 122888 | tf_op jit(solution)/shard_map/ppermute | solution.py:41
  23.3 0.0 collective-permute-start.8
  23.3 4.7 %collective-permute-done.9.refs_10_ = bf16[80,256]{1,0:T(8,128)(2,1)S(1)} collective-permute-done((bf16[80,256]{1,0:T(8,128)(2,1)S(1)}, bf16[80,256]{1,0:T(8,128)(2,1)S(1)}, u32[]{:S(2)}, u32[]{:S(2)}) %collective-permute-start.9) | collective-permute-done | bytes 40992 | tf_op jit(solution)/shard_map/ppermute | solution.py:41
  27.9 0.0 collective-permute-done.7.refs_8_
  27.9 0.0 collective-permute-done.5.refs_6_
  27.9 0.0 collective-permute-done.6.refs_7_
  28.0 2.6 %second.1 = (f32[16,8192]{1,0:T(8,128)}, f32[136,256]{1,0:T(8,128)S(1)}, f32[64,256]{1,0:T(8,128)S(1)}, bf16[144,256]{1,0:T(8,128)(2,1)S(1)}) custom-call(f32[16,16]{1,0:T(8,128)S(1)} %copy-done.5, f32[16,8192]{1,0:T(8,128)S(1)} %get-tuple-element.23.refs_1_, s32[2,8192]{1,0:T(2,128)S(1)} %get-tuple-element.20.refs_2_, ...), custom_call_target="tpu_custom_call" | custom-call | flops 4294967296 | bytes 1048576 | tf_op jit(solution)/shard_map/second/pallas_call | solution.py:442
  30.6 0.6 %collective-permute-start.10 = (bf16[144,256]{1,0:T(8,128)(2,1)S(1)}, bf16[144,256]{1,0:T(8,128)(2,1)S(1)}, u32[]{:S(2)}, u32[]{:S(2)}) collective-permute-start(bf16[144,256]{1,0:T(8,128)(2,1)S(1)} %get-tuple-element.31), channel_id=1, source_target_pairs={{0,16},{1,17},{2,18},{3,19},{4,20},{5,21},{6,22},{7,23},{8,24},{9,... | collective-permute-start | bytes 221192 | tf_op jit(solution)/shard_map/ppermute | solution.py:41
  31.2 3.8 %collective-permute-done.10.refs_2_ = bf16[144,256]{1,0:T(8,128)(2,1)S(1)} collective-permute-done((bf16[144,256]{1,0:T(8,128)(2,1)S(1)}, bf16[144,256]{1,0:T(8,128)(2,1)S(1)}, u32[]{:S(2)}, u32[]{:S(2)}) %collective-permute-start.10) | collective-permute-done | bytes 73760 | tf_op jit(solution)/shard_map/ppermute | solution.py:41
  35.0 0.7 %last.1 = (f32[8,2,1024]{2,1,0:T(2,128)}, f32[8,2,1024]{2,1,0:T(2,128)}) custom-call(f32[136,256]{1,0:T(8,128)S(1)} %get-tuple-element.29.refs_0_, f32[64,256]{1,0:T(8,128)S(1)} %get-tuple-element.30.refs_1_, bf16[144,256]{1,0:T(8,128)(2,1)S(1)} %collective-permute-done.10.refs_2_), custom_call_target="tpu_custom_call" | custom-call | flops 1048576 | bytes 1048576 | tf_op jit(solution)/shard_map/last/pallas_call | solution.py:442
  (12 shorter events, 0.1 us)
Async XLA Ops:
  0.6 9.4 %copy-start.6 = (f32[8,2,1024]{2,1,0:T(2,128)S(1)}, f32[8,2,1024]{2,1,0:T(2,128)}, u32[]{:S(2)}) copy-start(f32[8,2,1024]{2,1,0:T(2,128)} %param.7) | copy-start | bytes 196612
  1.6 8.5 %copy-start.1 = (s32[2,8192]{1,0:T(2,128)S(1)}, s32[2,8192]{1,0:T(2,128)}, u32[]{:S(2)}) copy-start(s32[2,8192]{1,0:T(2,128)} %cells.1) | copy-start | bytes 196612
  1.6 8.5 %copy-start.2 = (f32[2,1024]{1,0:T(2,128)S(1)}, f32[2,1024]{1,0:T(2,128)}, u32[]{:S(2)}) copy-start(f32[2,1024]{1,0:T(2,128)} %rate.1) | copy-start | bytes 24580
  1.6 8.5 %copy-start.3 = (s32[64]{0:T(128)S(1)}, s32[64]{0:T(128)}, u32[]{:S(2)}) copy-start(s32[64]{0:T(128)} %dest.1) | copy-start | bytes 772
  1.6 8.5 %copy-start.4 = (s32[64]{0:T(128)S(1)}, s32[64]{0:T(128)}, u32[]{:S(2)}) copy-start(s32[64]{0:T(128)} %counts.1) | copy-start | bytes 772
  1.6 10.7 %collective-permute-start.4 = (bf16[16,1024]{1,0:T(8,128)(2,1)S(1)}, bf16[16,1024]{1,0:T(8,128)(2,1)S(1)}, u32[]{:S(2)}, u32[]{:S(2)}) collective-permute-start(bf16[16,1024]{1,0:T(8,128)(2,1)S(1)} %bitcast.10), channel_id=1, source_target_pairs={{0,31},{1,18},{2,17},{3,20},{4,19},{5,22},{6,21},{7,24},{8,23},{9,... | collective-permute-start | bytes 98312 | tf_op jit(solution)/shard_map/ppermute | solution.py:41
  8.1 4.3 %collective-permute-start.3 = (bf16[16,1024]{1,0:T(8,128)(2,1)S(1)}, bf16[16,1024]{1,0:T(8,128)(2,1)S(1)}, u32[]{:S(2)}, u32[]{:S(2)}) collective-permute-start(bf16[16,1024]{1,0:T(8,128)(2,1)S(1)} %bitcast.11), channel_id=1, source_target_pairs={{0,17},{1,16},{2,19},{3,18},{4,21},{5,20},{6,23},{7,22},{8,25},{9,... | collective-permute-start | bytes 98312 | tf_op jit(solution)/shard_map/ppermute | solution.py:41
  8.1 4.3 %collective-permute-start.2 = (bf16[16,1024]{1,0:T(8,128)(2,1)S(1)}, bf16[16,1024]{1,0:T(8,128)(2,1)S(1)}, u32[]{:S(2)}, u32[]{:S(2)}) collective-permute-start(bf16[16,1024]{1,0:T(8,128)(2,1)S(1)} %bitcast.12), channel_id=1, source_target_pairs={{0,16},{1,17},{2,18},{3,19},{4,20},{5,21},{6,22},{7,23},{8,24},{9,... | collective-permute-start | bytes 98312 | tf_op jit(solution)/shard_map/ppermute | solution.py:41
  8.6 6.0 %collective-permute-start.1 = (bf16[16,1024]{1,0:T(8,128)(2,1)S(1)}, bf16[16,1024]{1,0:T(8,128)(2,1)S(1)}, u32[]{:S(2)}, u32[]{:S(2)}) collective-permute-start(bf16[16,1024]{1,0:T(8,128)(2,1)S(1)} %bitcast.13), channel_id=1, source_target_pairs={{0,15},{1,2},{2,1},{3,4},{4,3},{5,6},{6,5},{7,8},{8,7},{9,10},{10,... | collective-permute-start | bytes 98312 | tf_op jit(solution)/shard_map/ppermute | solution.py:41
  10.1 4.6 %collective-permute-start = (bf16[16,1024]{1,0:T(8,128)(2,1)S(1)}, bf16[16,1024]{1,0:T(8,128)(2,1)S(1)}, u32[]{:S(2)}, u32[]{:S(2)}) collective-permute-start(bf16[16,1024]{1,0:T(8,128)(2,1)S(1)} %bitcast.14), channel_id=1, source_target_pairs={{0,1},{1,0},{2,3},{3,2},{4,5},{5,4},{6,7},{7,6},{8,9},{9,8},{10,11... | collective-permute-start | bytes 98312 | tf_op jit(solution)/shard_map/ppermute | solution.py:41
  10.1 1.0 %copy-start = (f32[16,8192]{1,0:T(8,128)S(1)}, f32[16,8192]{1,0:T(8,128)}, u32[]{:S(2)}) copy-start(f32[16,8192]{1,0:T(8,128)} %particles.1) | copy-start | bytes 1572868
  12.3 2.3 %copy-start.5 = (f32[16,16]{1,0:T(8,128)S(1)}, f32[16,16]{1,0:T(8,128)}, u32[]{:S(2)}) copy-start(f32[16,16]{1,0:T(8,128)} %refs_0_.3) | copy-start | bytes 3076
  17.4 10.5 %collective-permute-start.5 = (bf16[224,256]{1,0:T(8,128)(2,1)S(1)}, bf16[224,256]{1,0:T(8,128)(2,1)S(1)}, u32[]{:S(2)}, u32[]{:S(2)}) collective-permute-start(bf16[224,256]{1,0:T(8,128)(2,1)S(1)} %get-tuple-element.26), channel_id=1, source_target_pairs={{0,1},{1,0},{2,3},{3,2},{4,5},{5,4},{6,7},{7,6},{8,9},{9,8},{10,11... | collective-permute-start | bytes 344072 | tf_op jit(solution)/shard_map/ppermute | solution.py:41
  17.5 10.5 %collective-permute-start.6 = (bf16[224,256]{1,0:T(8,128)(2,1)S(1)}, bf16[224,256]{1,0:T(8,128)(2,1)S(1)}, u32[]{:S(2)}, u32[]{:S(2)}) collective-permute-start(bf16[224,256]{1,0:T(8,128)(2,1)S(1)} %get-tuple-element.27), channel_id=1, source_target_pairs={{0,15},{1,2},{2,1},{3,4},{4,3},{5,6},{6,5},{7,8},{8,7},{9,10},{10,... | collective-permute-start | bytes 344072 | tf_op jit(solution)/shard_map/ppermute | solution.py:41
  19.3 8.6 %collective-permute-start.7 = (bf16[144,256]{1,0:T(8,128)(2,1)S(1)}, bf16[144,256]{1,0:T(8,128)(2,1)S(1)}, u32[]{:S(2)}, u32[]{:S(2)}) collective-permute-start(bf16[144,256]{1,0:T(8,128)(2,1)S(1)} %get-tuple-element.28), channel_id=1, source_target_pairs={{0,16},{1,17},{2,18},{3,19},{4,20},{5,21},{6,22},{7,23},{8,24},{9,... | collective-permute-start | bytes 221192 | tf_op jit(solution)/shard_map/ppermute | solution.py:41
  20.8 7.1 %collective-permute-start.9 = (bf16[80,256]{1,0:T(8,128)(2,1)S(1)}, bf16[80,256]{1,0:T(8,128)(2,1)S(1)}, u32[]{:S(2)}, u32[]{:S(2)}) collective-permute-start(bf16[80,256]{1,0:T(8,128)(2,1)S(1)} %slice.7), channel_id=1, source_target_pairs={{0,31},{1,18},{2,17},{3,20},{4,19},{5,22},{6,21},{7,24},{8,23},{9,... | collective-permute-start | bytes 122888 | tf_op jit(solution)/shard_map/ppermute | solution.py:41
  23.3 4.7 %collective-permute-start.8 = (bf16[80,256]{1,0:T(8,128)(2,1)S(1)}, bf16[80,256]{1,0:T(8,128)(2,1)S(1)}, u32[]{:S(2)}, u32[]{:S(2)}) collective-permute-start(bf16[80,256]{1,0:T(8,128)(2,1)S(1)} %slice.6), channel_id=1, source_target_pairs={{0,17},{1,16},{2,19},{3,18},{4,21},{5,20},{6,23},{7,22},{8,25},{9,... | collective-permute-start | bytes 122888 | tf_op jit(solution)/shard_map/ppermute | solution.py:41
  30.6 4.4 %collective-permute-start.10 = (bf16[144,256]{1,0:T(8,128)(2,1)S(1)}, bf16[144,256]{1,0:T(8,128)(2,1)S(1)}, u32[]{:S(2)}, u32[]{:S(2)}) collective-permute-start(bf16[144,256]{1,0:T(8,128)(2,1)S(1)} %get-tuple-element.31), channel_id=1, source_target_pairs={{0,16},{1,17},{2,18},{3,19},{4,20},{5,21},{6,22},{7,23},{8,24},{9,... | collective-permute-start | bytes 221192 | tf_op jit(solution)/shard_map/ppermute | solution.py:41

commit v3 on v2

--- a/solution.py
+++ b/solution.py
@@ -6,13 +6,12 @@
 from jax.experimental.pallas import tpu as pltpu
 from jax.sharding import PartitionSpec as P
 
+
 ROW_LENGTH = 32
 MOVE = 16
 BLOCK = 128
 LOW = 256
-SPAN = 4096
-UNROLL = True
-STEPS = 2
+SPAN = 8192
 SPLIT = 128.0
 
 NU_COEF = 0.15
@@ -31,10 +30,12 @@
     return (((s + 1) ^ 1) - 1) % n_sp
 
 
-def exchange(value, shift, pairing):
+def exchange(value, kind, shift):
     n_grp, n_sp = lax.axis_size("grp"), lax.axis_size("sp")
+    pairing = {"near": 0, "relay": 0, "far": 1, "same": None}[kind]
+    step = 0 if kind == "relay" else shift
     pairs = [
-        (g * n_sp + s, ((g + shift) % n_grp) * n_sp + partner(s, pairing, n_sp))
+        (g * n_sp + s, ((g + step) % n_grp) * n_sp + partner(s, pairing, n_sp))
         for g in range(n_grp)
         for s in range(n_sp)
     ]
@@ -122,12 +123,11 @@
 
 
 def advance(phi, codes, code_row, cells, table, reaction, n_parts, squares, mask_dead, out, sums):
-    spans = phi.shape[1] // SPAN
+    span = min(SPAN, phi.shape[1])
+    spans = phi.shape[1] // span
 
     def span_at(index):
-        if isinstance(index, int):
-            return slice(index * SPAN, (index + 1) * SPAN)
-        return pl.ds(pl.multiple_of(index * SPAN, SPAN), SPAN)
+        return slice(index * span, (index + 1) * span)
 
     def make(index):
         at = span_at(index)
@@ -141,23 +141,9 @@
 
     sums[...] = jnp.zeros_like(sums)
     make(0)
-    if UNROLL:
-        for index in range(1, spans):
-            make(index)
-            take(index - 1)
-    else:
-
-        def body(index, carry):
-            for step in range(STEPS):
-                make(STEPS * index + step + 1)
-                take(STEPS * index + step)
-            return carry
-
-        trips = (spans - 1) // STEPS
-        lax.fori_loop(0, trips, body, 0)
-        for index in range(trips * STEPS + 1, spans):
-            make(index)
-            take(index - 1)
+    for index in range(1, spans):
+        make(index)
+        take(index - 1)
     take(spans - 1)
 
 
@@ -317,11 +303,18 @@
         for pairing in range(2):
             message = received[position]
             position += 1
-            rows = message[: half + 2 * n_parts, :].astype(F32)
-            first = rows[:half]
-            count = rows[half : half + n_parts] * SPLIT + rows[half + n_parts :]
             if shift == 0:
                 moving[pairing] = message
+            if shift > 0 and pairing == 0:
+                rows = message[...].astype(F32)
+                first = jnp.where(even, rows[:half], rows[n_first - half : n_first])
+                rows = rows[n_first:]
+            else:
+                rows = message[: half + 2 * n_parts, :].astype(F32)
+                first = rows[:half]
+                rows = rows[half:]
+            count = rows[:n_parts] * SPLIT + rows[n_parts:]
+            if shift == 0:
                 side_first[pairing], side_count[pairing] = first, count
             else:
                 side_first[pairing] = side_first[pairing] + first
@@ -435,7 +428,7 @@
             ) * scale
 
 
-def call(kernel, name, outs, scratch, flops, smem=0, limit=20):
+def call(kernel, outs, scratch, flops, smem=0, limit=20):
     specs = [pl.BlockSpec(memory_space=pltpu.SMEM)] * smem
 
     def run(*args):
@@ -447,7 +440,6 @@
             scratch_shapes=[pltpu.VMEM(shape, dtype) for shape, dtype in scratch],
             compiler_params=pltpu.CompilerParams(vmem_limit_bytes=limit << 20),
             cost_estimate=pl.CostEstimate(flops=flops, bytes_accessed=1 << 20, transcendentals=0),
-            name=name,
         )(*args)
 
     return run
@@ -467,13 +459,12 @@
     sent = mine.astype(BF)
     fields = []
     for shift in range(n_grp):
+        near = exchange(sent, "near", shift)
         if shift > 0:
-            fields.append(exchange(sent, shift, None))
-        fields.append(exchange(sent, shift, 0))
-        fields.append(exchange(sent, shift, 1))
+            fields.append(exchange(near, "relay", shift))
+        fields += [near, exchange(sent, "far", shift)]
     sorted_phi, codes, cells_f, weights = call(
         order_kernel,
-        "order",
         [
             ((width, total), F32),
             ((2, total), jnp.int32),
@@ -490,7 +481,6 @@
     table = ((n_first + 2 * n_parts, LOW), BF)
     diffused0, sums0, slab_msg, pair0_msg, pair1_msg, stay_phi = call(
         functools.partial(first_kernel, n_grp, own),
-        "first",
         [
             (((depth + 2) * width, plane), F32),
             ((n_first + n_parts, LOW), F32),
@@ -504,17 +494,18 @@
     )(react, sorted_phi, codes, cells_f, weights, mine, *fields)
 
     received = []
-    faces = [message[: half + 2 * n_parts] for message in (pair0_msg, pair1_msg)]
     for shift in range(n_grp):
-        if shift > 0:
-            received.append(exchange(slab_msg, shift, None))
-        for pairing, message in enumerate((pair0_msg, pair1_msg)):
-            received.append(exchange(faces[pairing] if shift > 0 else message, shift, pairing))
+        if shift == 0:
+            received.append(exchange(pair0_msg, "near", 0))
+            received.append(exchange(pair1_msg, "far", 0))
+        else:
+            near = exchange(slab_msg, "near", shift)
+            received += [exchange(near, "relay", shift), near]
+            received.append(exchange(pair1_msg[: half + 2 * n_parts], "far", shift))
 
     n_own = 2 * n_parts * own
     outs = call(
         functools.partial(second_kernel, n_grp, own),
-        "second",
         [((width, total), F32), ((n_own + n_parts, LOW), F32), ((n_parts * own, LOW), F32)]
         + [((n_own + 2 * n_parts, LOW), BF)] * (n_grp - 1),
         [
@@ -528,10 +519,9 @@
         1 << 32,
     )(react, stay_phi, codes, weights, diffused0, sums0, *received)
     particles_out, own_sums, own_diffused = outs[:3]
-    final = [exchange(outs[2 + shift], shift, None) for shift in range(1, n_grp)]
+    final = [exchange(outs[2 + shift], "same", shift) for shift in range(1, n_grp)]
     field_out, spread_out = call(
         functools.partial(last_kernel, n_grp, own),
-        "last",
         [(field.shape, F32), (field.shape, F32)],
         [],
         1 << 20,

time: 35.9 us -> 37 us (1.031)
  waiting for transfers between devices: 10.8 us -> 12.6 us
  Pallas kernels: 7.2 us -> 6.78 us
    ppermute x11, waiting for transfers between devices: 10.8 us -> 12.6 us  [exchange(): return lax.ppermute(value, AXES, pairs)]
    pallas_call x4, Pallas kernels: 7.2 us -> 6.78 us  [run(): pl.pallas_call(kernel, out_shape=[jax.ShapeDtypeStruct(shape, dtype) for...]
  transfers between devices with their start and end apart: 11 -> 11, of which waited for: 3 -> 4; matrix products, arithmetic and copies ran while one was open for 0% -> 0% of each run, Pallas kernels for 3% -> 3%
where the time goes in v3:
time: 37 us; the launch traced here: 36.8 us
  starting transfers between devices  14.6 us (39%)
  waiting for transfers between devices  12.6 us (34%)
  Pallas kernels  6.78 us (18%)
  local copies, waits for them, and re-layouts  2.03 us (5%)
  between operations  0.77 us (2%)
    ppermute x11, starting transfers between devices, exchange(): return lax.ppermute(value, AXES, pairs)  14.6 us
    ppermute x11, waiting for transfers between devices, exchange(): return lax.ppermute(value, AXES, pairs)  12.6 us
    pallas_call x4, Pallas kernels, run(): pl.pallas_call(kernel, out_shape=[jax.ShapeDtypeStruct(shape, dtype) for...  6.78 us
    unnamed x14, local copies, waits for them, and re-layouts  1.07 us
    transpose x2, local copies, waits for them, and re-layouts, shards(): mine = jnp.transpose(field, (1, 0, 2)).reshape(depth * own, plane)  0.95 us
  transfers between devices with their start and end apart: 11, of which 4 were waited for; matrix products, arithmetic and copies ran while one was open for 0% of the time, Pallas kernels for 3%

profile of v3, /device:TPU:0, one launch (start us, length us, event | category | flops | bytes accessed | tf_op | source)
XLA Modules:
  0.0 36.8 jit_solution(6098442081057092066)
XLA Ops:
  0.6 0.9 %copy.15 = bf16[2,8,1024]{2,1,0:T(8,128)(2,1)S(1)} copy(f32[2,8,1024]{2,0,1:T(2,128)} %bitcast.8) | data formatting | bytes 98304 | tf_op jit(solution)/shard_map/transpose | solution.py:458
  1.6 0.0 copy-start.1
  1.6 0.0 copy-start.2
  1.6 0.0 copy-start.3
  1.6 0.0 copy-start.4
  1.6 2.5 %collective-permute-start.2 = (bf16[16,1024]{1,0:T(8,128)(2,1)S(1)}, bf16[16,1024]{1,0:T(8,128)(2,1)S(1)}, u32[]{:S(2)}, u32[]{:S(2)}) collective-permute-start(bf16[16,1024]{1,0:T(8,128)(2,1)S(1)} %bitcast.10), channel_id=1, source_target_pairs={{0,17},{1,16},{2,19},{3,18},{4,21},{5,20},{6,23},{7,22},{8,25},{9,... | collective-permute-start | bytes 98312 | tf_op jit(solution)/shard_map/ppermute | solution.py:42
  4.1 4.8 %collective-permute-start.4 = (bf16[16,1024]{1,0:T(8,128)(2,1)S(1)}, bf16[16,1024]{1,0:T(8,128)(2,1)S(1)}, u32[]{:S(2)}, u32[]{:S(2)}) collective-permute-start(bf16[16,1024]{1,0:T(8,128)(2,1)S(1)} %bitcast.11), channel_id=1, source_target_pairs={{0,31},{1,18},{2,17},{3,20},{4,19},{5,22},{6,21},{7,24},{8,23},{9,... | collective-permute-start | bytes 98312 | tf_op jit(solution)/shard_map/ppermute | solution.py:42
  8.9 0.0 collective-permute-start.1
  8.9 0.0 collective-permute-start
  8.9 0.0 collective-permute-done.2.refs_9_
  8.9 0.5 %collective-permute-start.3 = (bf16[16,1024]{1,0:T(8,128)(2,1)S(1)}, bf16[16,1024]{1,0:T(8,128)(2,1)S(1)}, u32[]{:S(2)}, u32[]{:S(2)}) collective-permute-start(bf16[16,1024]{1,0:T(8,128)(2,1)S(1)} %collective-permute-done.2.refs_9_), channel_id=1, source_target_pairs={{0,1},{1,0},{2,3},{3,2},{4,5},{5,4},{6,7},{7,6},{8,9},{9,8},{10,11... | collective-permute-start | bytes 98312 | tf_op jit(solution)/shard_map/ppermute | solution.py:42
  9.5 0.0 copy-start
  9.5 1.0 %copy-done = f32[16,8192]{1,0:T(8,128)S(1)} copy-done((f32[16,8192]{1,0:T(8,128)S(1)}, f32[16,8192]{1,0:T(8,128)}, u32[]{:S(2)}) %copy-start) | copy-done | bytes 524312
  10.6 1.1 %shard_map.94 = (f32[16,8192]{1,0:T(8,128)S(1)}, s32[2,8192]{1,0:T(2,128)S(1)}, f32[1,8192]{1,0:T(1,128)S(1)}, bf16[16,256]{1,0:T(8,128)(2,1)S(1)}) custom-call(s32[64]{0:T(128)S(1)} %copy-done.3, s32[64]{0:T(128)S(1)} %copy-done.4, f32[16,8192]{1,0:T(8,128)S(1)} %copy-done, s32[2,8192]{1,0:T(2,128)S(1)} %copy-done.1, f32[2,1024]{1,0:T(2,128)S(1)} %copy-done.2), custom_call_target="tpu_custom_call" | custom-call | flops 16777216 | bytes 1048576 | tf_op jit(solution)/shard_map/pallas_call | solution.py:435
  11.7 0.0 copy-start.5
  11.7 0.0 collective-permute-done.4.refs_10_
  11.7 3.2 %collective-permute-done.1.refs_7_ = bf16[16,1024]{1,0:T(8,128)(2,1)S(1)} collective-permute-done((bf16[16,1024]{1,0:T(8,128)(2,1)S(1)}, bf16[16,1024]{1,0:T(8,128)(2,1)S(1)}, u32[]{:S(2)}, u32[]{:S(2)}) %collective-permute-start.1) | collective-permute-done | bytes 32800 | tf_op jit(solution)/shard_map/ppermute | solution.py:42
  14.9 0.0 collective-permute-done.refs_6_
  14.9 0.0 collective-permute-done.3.refs_8_
  14.9 2.5 %shard_map.95 = (f32[64,1024]{1,0:T(8,128)S(1)}, f32[136,256]{1,0:T(8,128)S(1)}, bf16[144,256]{1,0:T(8,128)(2,1)S(1)}, bf16[224,256]{1,0:T(8,128)(2,1)S(1)}, bf1...) custom-call(f32[16,16]{1,0:T(8,128)S(1)} %copy-done.5, f32[16,8192]{1,0:T(8,128)S(1)} %get-tuple-element.19.refs_1_, ...), custom_call_target="tpu_custom_call" | custom-call | flops 4294967296 | bytes 1048576 | tf_op jit(solution)/shard_map/pallas_call | solution.py:435
  17.5 0.1 collective-permute-start.7
  17.5 1.6 %collective-permute-start.5 = (bf16[224,256]{1,0:T(8,128)(2,1)S(1)}, bf16[224,256]{1,0:T(8,128)(2,1)S(1)}, u32[]{:S(2)}, u32[]{:S(2)}) collective-permute-start(bf16[224,256]{1,0:T(8,128)(2,1)S(1)} %get-tuple-element.26), channel_id=1, source_target_pairs={{0,1},{1,0},{2,3},{3,2},{4,5},{5,4},{6,7},{7,6},{8,9},{9,8},{10,11... | collective-permute-start | bytes 344072 | tf_op jit(solution)/shard_map/ppermute | solution.py:42
  19.1 1.9 %collective-permute-start.6 = (bf16[224,256]{1,0:T(8,128)(2,1)S(1)}, bf16[224,256]{1,0:T(8,128)(2,1)S(1)}, u32[]{:S(2)}, u32[]{:S(2)}) collective-permute-start(bf16[224,256]{1,0:T(8,128)(2,1)S(1)} %get-tuple-element.27), channel_id=1, source_target_pairs={{0,15},{1,2},{2,1},{3,4},{4,3},{5,6},{6,5},{7,8},{8,7},{9,10},{10,... | collective-permute-start | bytes 344072 | tf_op jit(solution)/shard_map/ppermute | solution.py:42
  21.0 1.1 %collective-permute-done.7.refs_9_ = bf16[144,256]{1,0:T(8,128)(2,1)S(1)} collective-permute-done((bf16[144,256]{1,0:T(8,128)(2,1)S(1)}, bf16[144,256]{1,0:T(8,128)(2,1)S(1)}, u32[]{:S(2)}, u32[]{:S(2)}) %collective-permute-start.7) | collective-permute-done | bytes 73760 | tf_op jit(solution)/shard_map/ppermute | solution.py:42
  22.1 0.1 collective-permute-start.8
  22.2 2.4 %collective-permute-start.9 = (bf16[80,256]{1,0:T(8,128)(2,1)S(1)}, bf16[80,256]{1,0:T(8,128)(2,1)S(1)}, u32[]{:S(2)}, u32[]{:S(2)}) collective-permute-start(bf16[80,256]{1,0:T(8,128)(2,1)S(1)} %slice.3), channel_id=1, source_target_pairs={{0,31},{1,18},{2,17},{3,20},{4,19},{5,22},{6,21},{7,24},{8,23},{9,... | collective-permute-start | bytes 122888 | tf_op jit(solution)/shard_map/ppermute | solution.py:42
  24.6 4.6 %collective-permute-done.9.refs_10_ = bf16[80,256]{1,0:T(8,128)(2,1)S(1)} collective-permute-done((bf16[80,256]{1,0:T(8,128)(2,1)S(1)}, bf16[80,256]{1,0:T(8,128)(2,1)S(1)}, u32[]{:S(2)}, u32[]{:S(2)}) %collective-permute-start.9) | collective-permute-done | bytes 40992 | tf_op jit(solution)/shard_map/ppermute | solution.py:42
  29.2 0.0 collective-permute-done.5.refs_6_
  29.2 2.4 %shard_map.96 = (f32[16,8192]{1,0:T(8,128)}, f32[136,256]{1,0:T(8,128)S(1)}, f32[64,256]{1,0:T(8,128)S(1)}, bf16[144,256]{1,0:T(8,128)(2,1)S(1)}) custom-call(f32[16,16]{1,0:T(8,128)S(1)} %copy-done.5, f32[16,8192]{1,0:T(8,128)S(1)} %get-tuple-element.23.refs_1_, s32[2,8192]{1,0:T(2,128)S(1)} %get-tuple-element.20.refs_2_, ...), custom_call_target="tpu_custom_call" | custom-call | flops 4294967296 | bytes 1048576 | tf_op jit(solution)/shard_map/pallas_call | solution.py:435
  31.6 0.8 %collective-permute-start.10 = (bf16[144,256]{1,0:T(8,128)(2,1)S(1)}, bf16[144,256]{1,0:T(8,128)(2,1)S(1)}, u32[]{:S(2)}, u32[]{:S(2)}) collective-permute-start(bf16[144,256]{1,0:T(8,128)(2,1)S(1)} %get-tuple-element.31), channel_id=1, source_target_pairs={{0,16},{1,17},{2,18},{3,19},{4,20},{5,21},{6,22},{7,23},{8,24},{9,... | collective-permute-start | bytes 221192 | tf_op jit(solution)/shard_map/ppermute | solution.py:42
  32.4 3.7 %collective-permute-done.10.refs_2_ = bf16[144,256]{1,0:T(8,128)(2,1)S(1)} collective-permute-done((bf16[144,256]{1,0:T(8,128)(2,1)S(1)}, bf16[144,256]{1,0:T(8,128)(2,1)S(1)}, u32[]{:S(2)}, u32[]{:S(2)}) %collective-permute-start.10) | collective-permute-done | bytes 73760 | tf_op jit(solution)/shard_map/ppermute | solution.py:42
  36.0 0.7 %shard_map.97 = (f32[8,2,1024]{2,1,0:T(2,128)}, f32[8,2,1024]{2,1,0:T(2,128)}) custom-call(f32[136,256]{1,0:T(8,128)S(1)} %get-tuple-element.29.refs_0_, f32[64,256]{1,0:T(8,128)S(1)} %get-tuple-element.30.refs_1_, bf16[144,256]{1,0:T(8,128)(2,1)S(1)} %collective-permute-done.10.refs_2_), custom_call_target="tpu_custom_call" | custom-call | flops 1048576 | bytes 1048576 | tf_op jit(solution)/shard_map/pallas_call | solution.py:435
  (11 shorter events, 0.0 us)
Async XLA Ops:
  0.6 8.8 %copy-start.6 = (f32[8,2,1024]{2,1,0:T(2,128)S(1)}, f32[8,2,1024]{2,1,0:T(2,128)}, u32[]{:S(2)}) copy-start(f32[8,2,1024]{2,1,0:T(2,128)} %param.7) | copy-start | bytes 196612
  1.6 7.9 %copy-start.1 = (s32[2,8192]{1,0:T(2,128)S(1)}, s32[2,8192]{1,0:T(2,128)}, u32[]{:S(2)}) copy-start(s32[2,8192]{1,0:T(2,128)} %cells.1) | copy-start | bytes 196612
  1.6 7.9 %copy-start.2 = (f32[2,1024]{1,0:T(2,128)S(1)}, f32[2,1024]{1,0:T(2,128)}, u32[]{:S(2)}) copy-start(f32[2,1024]{1,0:T(2,128)} %rate.1) | copy-start | bytes 24580
  1.6 7.9 %copy-start.3 = (s32[64]{0:T(128)S(1)}, s32[64]{0:T(128)}, u32[]{:S(2)}) copy-start(s32[64]{0:T(128)} %dest.1) | copy-start | bytes 772
  1.6 7.9 %copy-start.4 = (s32[64]{0:T(128)S(1)}, s32[64]{0:T(128)}, u32[]{:S(2)}) copy-start(s32[64]{0:T(128)} %counts.1) | copy-start | bytes 772
  1.6 7.3 %collective-permute-start.2 = (bf16[16,1024]{1,0:T(8,128)(2,1)S(1)}, bf16[16,1024]{1,0:T(8,128)(2,1)S(1)}, u32[]{:S(2)}, u32[]{:S(2)}) collective-permute-start(bf16[16,1024]{1,0:T(8,128)(2,1)S(1)} %bitcast.10), channel_id=1, source_target_pairs={{0,17},{1,16},{2,19},{3,18},{4,21},{5,20},{6,23},{7,22},{8,25},{9,... | collective-permute-start | bytes 98312 | tf_op jit(solution)/shard_map/ppermute | solution.py:42
  4.1 7.6 %collective-permute-start.4 = (bf16[16,1024]{1,0:T(8,128)(2,1)S(1)}, bf16[16,1024]{1,0:T(8,128)(2,1)S(1)}, u32[]{:S(2)}, u32[]{:S(2)}) collective-permute-start(bf16[16,1024]{1,0:T(8,128)(2,1)S(1)} %bitcast.11), channel_id=1, source_target_pairs={{0,31},{1,18},{2,17},{3,20},{4,19},{5,22},{6,21},{7,24},{8,23},{9,... | collective-permute-start | bytes 98312 | tf_op jit(solution)/shard_map/ppermute | solution.py:42
  8.9 6.0 %collective-permute-start.1 = (bf16[16,1024]{1,0:T(8,128)(2,1)S(1)}, bf16[16,1024]{1,0:T(8,128)(2,1)S(1)}, u32[]{:S(2)}, u32[]{:S(2)}) collective-permute-start(bf16[16,1024]{1,0:T(8,128)(2,1)S(1)} %bitcast.12), channel_id=1, source_target_pairs={{0,15},{1,2},{2,1},{3,4},{4,3},{5,6},{6,5},{7,8},{8,7},{9,10},{10,... | collective-permute-start | bytes 98312 | tf_op jit(solution)/shard_map/ppermute | solution.py:42
  8.9 6.0 %collective-permute-start = (bf16[16,1024]{1,0:T(8,128)(2,1)S(1)}, bf16[16,1024]{1,0:T(8,128)(2,1)S(1)}, u32[]{:S(2)}, u32[]{:S(2)}) collective-permute-start(bf16[16,1024]{1,0:T(8,128)(2,1)S(1)} %bitcast.13), channel_id=1, source_target_pairs={{0,1},{1,0},{2,3},{3,2},{4,5},{5,4},{6,7},{7,6},{8,9},{9,8},{10,11... | collective-permute-start | bytes 98312 | tf_op jit(solution)/shard_map/ppermute | solution.py:42
  8.9 6.0 %collective-permute-start.3 = (bf16[16,1024]{1,0:T(8,128)(2,1)S(1)}, bf16[16,1024]{1,0:T(8,128)(2,1)S(1)}, u32[]{:S(2)}, u32[]{:S(2)}) collective-permute-start(bf16[16,1024]{1,0:T(8,128)(2,1)S(1)} %collective-permute-done.2.refs_9_), channel_id=1, source_target_pairs={{0,1},{1,0},{2,3},{3,2},{4,5},{5,4},{6,7},{7,6},{8,9},{9,8},{10,11... | collective-permute-start | bytes 98312 | tf_op jit(solution)/shard_map/ppermute | solution.py:42
  9.5 1.0 %copy-start = (f32[16,8192]{1,0:T(8,128)S(1)}, f32[16,8192]{1,0:T(8,128)}, u32[]{:S(2)}) copy-start(f32[16,8192]{1,0:T(8,128)} %particles.1) | copy-start | bytes 1572868
  11.7 3.2 %copy-start.5 = (f32[16,16]{1,0:T(8,128)S(1)}, f32[16,16]{1,0:T(8,128)}, u32[]{:S(2)}) copy-start(f32[16,16]{1,0:T(8,128)} %refs_0_.3) | copy-start | bytes 3076
  17.5 4.6 %collective-permute-start.7 = (bf16[144,256]{1,0:T(8,128)(2,1)S(1)}, bf16[144,256]{1,0:T(8,128)(2,1)S(1)}, u32[]{:S(2)}, u32[]{:S(2)}) collective-permute-start(bf16[144,256]{1,0:T(8,128)(2,1)S(1)} %get-tuple-element.28), channel_id=1, source_target_pairs={{0,17},{1,16},{2,19},{3,18},{4,21},{5,20},{6,23},{7,22},{8,25},{9,... | collective-permute-start | bytes 221192 | tf_op jit(solution)/shard_map/ppermute | solution.py:42
  17.5 11.7 %collective-permute-start.5 = (bf16[224,256]{1,0:T(8,128)(2,1)S(1)}, bf16[224,256]{1,0:T(8,128)(2,1)S(1)}, u32[]{:S(2)}, u32[]{:S(2)}) collective-permute-start(bf16[224,256]{1,0:T(8,128)(2,1)S(1)} %get-tuple-element.26), channel_id=1, source_target_pairs={{0,1},{1,0},{2,3},{3,2},{4,5},{5,4},{6,7},{7,6},{8,9},{9,8},{10,11... | collective-permute-start | bytes 344072 | tf_op jit(solution)/shard_map/ppermute | solution.py:42
  19.1 10.1 %collective-permute-start.6 = (bf16[224,256]{1,0:T(8,128)(2,1)S(1)}, bf16[224,256]{1,0:T(8,128)(2,1)S(1)}, u32[]{:S(2)}, u32[]{:S(2)}) collective-permute-start(bf16[224,256]{1,0:T(8,128)(2,1)S(1)} %get-tuple-element.27), channel_id=1, source_target_pairs={{0,15},{1,2},{2,1},{3,4},{4,3},{5,6},{6,5},{7,8},{8,7},{9,10},{10,... | collective-permute-start | bytes 344072 | tf_op jit(solution)/shard_map/ppermute | solution.py:42
  22.1 7.2 %collective-permute-start.8 = (bf16[144,256]{1,0:T(8,128)(2,1)S(1)}, bf16[144,256]{1,0:T(8,128)(2,1)S(1)}, u32[]{:S(2)}, u32[]{:S(2)}) collective-permute-start(bf16[144,256]{1,0:T(8,128)(2,1)S(1)} %collective-permute-done.7.refs_9_), channel_id=1, source_target_pairs={{0,1},{1,0},{2,3},{3,2},{4,5},{5,4},{6,7},{7,6},{8,9},{9,8},{10,11... | collective-permute-start | bytes 221192 | tf_op jit(solution)/shard_map/ppermute | solution.py:42
  22.2 7.0 %collective-permute-start.9 = (bf16[80,256]{1,0:T(8,128)(2,1)S(1)}, bf16[80,256]{1,0:T(8,128)(2,1)S(1)}, u32[]{:S(2)}, u32[]{:S(2)}) collective-permute-start(bf16[80,256]{1,0:T(8,128)(2,1)S(1)} %slice.3), channel_id=1, source_target_pairs={{0,31},{1,18},{2,17},{3,20},{4,19},{5,22},{6,21},{7,24},{8,23},{9,... | collective-permute-start | bytes 122888 | tf_op jit(solution)/shard_map/ppermute | solution.py:42
  31.6 4.4 %collective-permute-start.10 = (bf16[144,256]{1,0:T(8,128)(2,1)S(1)}, bf16[144,256]{1,0:T(8,128)(2,1)S(1)}, u32[]{:S(2)}, u32[]{:S(2)}) collective-permute-start(bf16[144,256]{1,0:T(8,128)(2,1)S(1)} %get-tuple-element.31), channel_id=1, source_target_pairs={{0,16},{1,17},{2,18},{3,19},{4,20},{5,21},{6,22},{7,23},{8,24},{9,... | collective-permute-start | bytes 221192 | tf_op jit(solution)/shard_map/ppermute | solution.py:42
